TPU v7x, 128 devices: a whole 4x4x4 slice. The times are simulated.
128 devices in a mesh: dp: 16 (over x_hi, z, core), tensor: 8 (over x_lo, y).
Axes of the slice: x: 4 (x_hi: 2, x_lo: 2; x = x_hi * 2 + x_lo), y: 4, z: 4, core: 2. Of those that a mesh axis runs over, the one named last changes fastest.
Arguments:
- tokens: bfloat16 [20480, 4096], P(('dp', 'tensor')), parts along dimension 0, may hold values from -6 to 6
- norm_gain: bfloat16 [4096], replicated, may hold values from 0.099609375 to 1.8984375
- query_weight: bfloat16 [4096, 8192], P(None, 'tensor'), may hold values from -0.09375 to 0.09375
- key_weight: bfloat16 [4096, 1024], P(None, 'tensor'), may hold values from -0.09375 to 0.09375
- value_weight: bfloat16 [4096, 1024], P(None, 'tensor'), may hold values from -0.09375 to 0.09375
- out_weight: bfloat16 [8192, 4096], P('tensor'), may hold values from -0.0625 to 0.0625
- past_cache: bfloat16 [2048, 64, 2, 1024], P('dp', None, None, 'tensor'), parts along dimension 0, may hold values from -320 to 320
- exponents: int32 [20480, 32], P('dp'), parts along dimension 0, may hold values from -11 to -7
Outputs:
- mixed: bfloat16 [20480, 4096], P(('dp', 'tensor')), parts along dimension 0
There are 16 independent parts, one for each index of `dp`. A program takes and returns all parts, laid end to end along the dimension named above; an argument that names none is the same for every part. Nothing has to cross between parts.
All inputs are finite; a program needn't handle non-finite values.
Results may differ from a plain program's by a relative error of at most 0.012.
The roundings to bfloat16 on the way count: a program that leaves them out, or rounds other values in their place, can miss the bound.
Values may be sent and summed in bfloat16 or wider, within the bound.
No kernel may reach another device: no remote copies, remote signals or barrier semaphores. Data moves between devices by JAX's collectives and lax.ppermute only.
A program may use at most 192 MiB of HBM per device.

v0:
```python
import jax
import jax.numpy as jnp
from jax import lax
from jax.sharding import PartitionSpec as P

HD = 128
NEW = 10
CACHE = 64


epsilon = 1e-05
theta_base = 500000.0


def in_order(pieces, dim):
    pieces = jnp.moveaxis(pieces, 0, dim)
    dims = pieces.shape
    return pieces.reshape(*dims[:dim], dims[dim] * dims[dim + 1], *dims[dim + 2 :])


def work_in_pieces(x, axis, dim, apply, out_dim):
    size, width = (lax.axis_size(axis), x.shape[dim])
    count = 2 if width % 2 == 0 else 1
    finished, length = ([], width // count)
    for k in range(count):
        share = lax.slice_in_dim(x, k * length, (k + 1) * length, axis=dim)
        starts = jnp.arange(size) * width + k * length
        finished.append(jax.vmap(apply)(lax.all_gather(share, axis), starts))
    return in_order(jnp.concatenate(finished, axis=out_dim + 1), out_dim)


def rotate(matrix, heads):
    row_count = matrix.shape[0]
    half_dim = HD // 2
    positions = (jnp.arange(row_count, dtype=jnp.int32) % NEW + CACHE).astype(jnp.float32)
    frequency = theta_base ** (-(jnp.arange(half_dim, dtype=jnp.float32) * 2.0) / HD)
    angles = positions[:, None] * frequency[None, :]
    cosine = jnp.cos(angles)[:, None, :]
    sine_part = jnp.sin(angles)[:, None, :]
    shaped = matrix.reshape(row_count, heads, 2, half_dim)
    first = shaped[:, :, 0]
    second = shaped[:, :, 1]
    turned = jnp.stack(
        [first * cosine - second * sine_part, second * cosine + first * sine_part], 2
    )
    return turned.reshape(row_count, heads * HD)


def attention(query, key_new, value_new, past_cache, kv_heads):
    row_count = query.shape[0]
    seq_count = row_count // NEW
    group_size = query.shape[1] // (kv_heads * HD)
    cache_len = past_cache.shape[1]
    query_heads = query.reshape(seq_count, NEW, kv_heads, group_size, HD)
    new_keys = key_new.reshape(seq_count, NEW, kv_heads, HD)
    new_values = value_new.reshape(seq_count, NEW, kv_heads, HD)
    cache_keys = past_cache[:, :, 0].reshape(seq_count, cache_len, kv_heads, HD)
    cache_values = past_cache[:, :, 1].reshape(seq_count, cache_len, kv_heads, HD)
    inv_root = 1.0 / HD**0.5
    cache_scores = (
        jnp.einsum("stkgd,sckd->skgtc", query_heads, cache_keys, preferred_element_type=jnp.float32)
        * inv_root
    )
    new_scores = (
        jnp.einsum("stkgd,sukd->skgtu", query_heads, new_keys, preferred_element_type=jnp.float32)
        * inv_root
    )
    causal = jnp.arange(NEW)[:, None] >= jnp.arange(NEW)[None, :]
    new_scores = jnp.where(causal, new_scores, -1e30)
    row_max = jnp.maximum(cache_scores.max(-1), new_scores.max(-1))[..., None]
    cache_probs = jnp.exp(cache_scores - row_max)
    new_probs = jnp.exp(new_scores - row_max)
    denominator = (cache_probs.sum(-1) + new_probs.sum(-1))[..., None]
    cache_weights = (cache_probs / denominator).astype(jnp.bfloat16)
    new_weights = (new_probs / denominator).astype(jnp.bfloat16)
    combined = jnp.einsum(
        "skgtc,sckd->stkgd", cache_weights, cache_values, preferred_element_type=jnp.float32
    )
    combined = combined + jnp.einsum(
        "skgtu,sukd->stkgd", new_weights, new_values, preferred_element_type=jnp.float32
    )
    return combined.reshape(row_count, kv_heads * group_size * HD).astype(jnp.bfloat16)


def on_device(
    tokens, norm_gain, query_weight, key_weight, value_weight, out_weight, past_cache, exponents
):
    kv_local = key_weight.shape[1] // HD
    query_local = query_weight.shape[1] // HD
    query_cols = query_weight.shape[1]
    key_cols = key_weight.shape[1]
    gain_f32 = norm_gain.astype(jnp.float32)

    def project(block_rows, offset):
        floats = block_rows.astype(jnp.float32)
        normed = floats * lax.rsqrt(jnp.mean(floats * floats, axis=-1, keepdims=True) + epsilon)
        normed = (normed * gain_f32).astype(jnp.bfloat16)
        return jnp.concatenate(
            [
                jnp.dot(normed, query_weight, preferred_element_type=jnp.float32),
                jnp.dot(normed, key_weight, preferred_element_type=jnp.float32),
                jnp.dot(normed, value_weight, preferred_element_type=jnp.float32),
            ],
            1,
        )

    projected = work_in_pieces(tokens, "tensor", 0, project, 0)
    query = rotate(projected[:, :query_cols], query_local).astype(jnp.bfloat16)
    key_new = rotate(projected[:, query_cols : query_cols + key_cols], kv_local).astype(
        jnp.bfloat16
    )
    value_new = projected[:, query_cols + key_cols :].astype(jnp.bfloat16)
    attended = attention(query, key_new, value_new, past_cache, kv_local)
    partial_value = jnp.dot(attended, out_weight, preferred_element_type=jnp.float32)
    row_count = partial_value.shape[0]
    groups = exponents.shape[1]
    shrink = jnp.exp2(-exponents.astype(jnp.float32))[..., None]
    scaled = jnp.clip(partial_value.reshape(row_count, groups, -1) * shrink, -127.0, 127.0)
    rounded = lax.optimization_barrier(scaled.astype(jnp.bfloat16)).astype(jnp.float32)
    rounded = rounded.reshape(row_count, -1)
    own_rows = row_count // lax.axis_size("tensor")
    share = lax.psum_scatter(
        rounded.astype(jnp.bfloat16), "tensor", scatter_dimension=0, tiled=True
    ).astype(jnp.float32)
    own_exponents = lax.dynamic_slice_in_dim(
        exponents, lax.axis_index("tensor") * own_rows, own_rows, 0
    )
    restore = jnp.exp2(own_exponents.astype(jnp.float32))[..., None]
    layer_out = tokens.astype(jnp.float32) + (
        share.reshape(own_rows, groups, -1) * restore
    ).reshape(own_rows, -1)
    return layer_out.astype(jnp.bfloat16)


def solution(mesh):
    return jax.shard_map(
        on_device,
        mesh=mesh,
        in_specs=(
            P(("dp", "tensor"), None),
            P(),
            P(None, "tensor"),
            P(None, "tensor"),
            P(None, "tensor"),
            P("tensor", None),
            P("dp", None, None, "tensor"),
            P("dp", None),
        ),
        out_specs=P(("dp", "tensor"), None),
        check_vma=False,
    )
```

profile of v0, /device:TPU:1, one launch (start us, length us, event | category | flops | bytes accessed | tf_op | source)
XLA Modules:
  0.0 435.2 jit_solution(7827488118867053869)
XLA Ops:
  6.5 2.6 fusion.66
  9.1 0.0 all-gather.5.cloned.1.call-update
  9.1 0.0 all-gather.7.cloned.1.call-start
  9.2 0.7 all-gather.7.cloned.1.call-update
  9.9 0.0 reduce-scatter.4.cloned.1.call-start
  9.9 0.7 convert_element_type.94
  10.6 12.0 %copy.95 = bf16[4096,1024]{1,0:T(8,128)(2,1)} copy(bf16[4096,1024]{0,1:T(8,128)(2,1)} %bitcast.113) | data formatting | bytes 16777216 | tf_op jit(solution)/shard_map/dot_general | solution.py:114
  22.7 0.7 multiply_exponential_fusion
  23.4 1.2 multiply_cosine_fusion.1
  24.6 15.5 %fusion.65 = (bf16[128,64,1,128]{3,2,1,0:T(2,128)(2,1)}, bf16[128,64,1,128]{3,2,1,0:T(2,128)(2,1)}) fusion(bf16[128,64,2,128]{3,2,1,0:T(2,128)(2,1)} %param.14), kind=kLoop, calls=%fused_computation.90 | loop fusion | bytes 8388608 | tf_op jit(solution)/shard_map/slice | solution.py:58
  40.2 34.5 %all-gather.5.cloned.1.call-done = bf16[640,4096]{1,0:T(8,128)(2,1)} async-done(((bf16[80,4096]{1,0:T(8,128)(2,1)}), bf16[640,4096]{1,0:T(8,128)(2,1)}) %all-gather.5.cloned.1.call-update) | async-done | bytes 5242896 | tf_op jit(solution)/shard_map/all_gather | solution.py:28
  74.7 3.6 fusion.2
  78.3 59.2 %all-gather.7.cloned.1.call-done = bf16[640,4096]{1,0:T(8,128)(2,1)} async-done(((bf16[80,4096]{1,0:T(8,128)(2,1)}), bf16[640,4096]{1,0:T(8,128)(2,1)}) %all-gather.7.cloned.1.call-update) | async-done | bytes 5242896 | tf_op jit(solution)/shard_map/all_gather | solution.py:28
  137.5 3.7 fusion.5
  141.2 0.3 copy-done.5
  141.5 9.4 %fusion.11 = f32[8,80,1024]{2,1,0:T(8,128)S(1)} fusion(bf16[4096,1024]{1,0:T(8,128)(2,1)} %param.10, bf16[8,80,4096]{2,1,0:T(8,128)(2,1)S(1)} %bitcast.116, f32[4096]{0:T(1024)S(1)} %convert_element_type.94, f32[8,80]{1,0:T(8,128)S(1)} %add_rsqrt_fusion.1), kind=kOutput, calls=%fused_computation.18 | convolution fusion | flops 5379194880 | bytes 16271872 | tf_op jit(solution)/shard_map/vmap()/dot_general | solution.py:100
  150.9 0.0 slice-done
  151.0 5.7 %fusion.9 = f32[8,80,1024]{2,1,0:T(8,128)S(1)} fusion(bf16[4096,1024]{1,0:T(8,128)(2,1)S(1)} %bitcast.127, bf16[8,80,4096]{2,1,0:T(8,128)(2,1)S(1)} %bitcast.122, f32[8,80]{1,0:T(8,128)S(1)} %add_rsqrt_fusion, f32[4096]{0:T(1024)S(1)} %convert_element_type.94), kind=kOutput, calls=%fused_computation.16 | convolution fusion | flops 5379194880 | bytes 16271872 | tf_op jit(solution)/shard_map/vmap()/dot_general | solution.py:100
  156.7 1.6 fusion.28
  158.3 0.0 copy-start.9
  158.3 1.6 fusion.33
  159.9 1.6 fusion.30
  161.5 1.6 fusion.35
  163.1 0.6 maximum_maximum_fusion
  163.7 3.4 slice.45
  167.1 1.0 copy-done.2
  168.1 5.9 %copy.98 = f32[1280,1024]{0,1:T(8,128)} copy(f32[1280,1024]{1,0:T(8,128)} %slice.45) | data formatting | bytes 10485760
  174.1 3.2 subtract_convert_fusion
  177.3 1.7 pad_maximum_fusion
  179.1 11.7 %copy.69 = bf16[1280,8,2,64]{3,2,1,0:T(2,128)(2,1)} copy(bf16[1280,8,2,64]{0,3,2,1:T(8,128)(2,1)} %pad_maximum_fusion) | data formatting | bytes 5242880 | tf_op jit(solution)/shard_map/stack | solution.py:43
  190.7 9.3 %convert_element_type.99 = bf16[128,10,8,128]{3,2,1,0:T(8,128)(2,1)} reshape(bf16[1280,8,2,64]{3,2,1,0:T(2,128)(2,1)} %copy.69) | data formatting | bytes 5242880 | tf_op jit(solution)/shard_map/convert_element_type | solution.py:108
  200.1 6.8 %bitcast_reduce_fusion = (f32[128,8,10]{1,2,0:T(8,128)S(1)}, f32[128,10,8,64]{3,2,1,0:T(8,128)}) fusion(bf16[128,10,8,128]{3,2,1,0:T(8,128)(2,1)} %convert_element_type.99, bf16[128,64,1,128]{3,2,1,0:T(2,128)(2,1)} %get-tuple-element.8), kind=kOutput, calls=%fused_computation.26 | convolution fusion | flops 169072640 | bytes 7380992 | tf_op jit(solution)/shard_map/stkgd,sckd->skgtc/dot_general | solution.py:61
  206.9 0.3 copy.74
  207.2 0.2 copy.100
  207.4 1.4 fusion.55
  208.9 0.5 copy.72
  209.4 0.4 reshape.280
  209.7 15.0 %fusion.14 = (f32[128,8,10]{2,1,0:T(8,128)S(1)}, f32[128,10,10,8]{2,1,3,0:T(8,128)}) fusion(pred[10,10]{0,1:T(8,128)(4,1)S(1)} %iota_compare_fusion, bf16[128,10,8,128]{3,2,1,0:T(8,128)(2,1)} %convert_element_type.99, bf16[128,10,128,1]{2,1,0,3:T(8,128)(2,1)S(1)} %reshape.280), kind=kOutput, calls=%fused_computation.24 | convolution fusion | flops 26511360 | bytes 3399780 | tf_op jit(solution)/shard_map/stkgd,sukd->skgtu/dot_general | solution.py:65
  224.7 0.2 copy.75
  224.9 0.3 copy.77
  225.2 0.5 copy.76
  225.7 5.4 %fusion.13 = f32[128,8,10]{2,1,0:T(8,128)S(1)} fusion(f32[128,10,10,8]{2,1,3,0:T(8,128)} %get-tuple-element.18, f32[128,8,10]{2,1,0:T(8,128)S(1)} %copy.77, pred[10,10]{0,1:T(8,128)(4,1)S(1)} %iota_compare_fusion), kind=kLoop, calls=%fused_computation.22 | loop fusion | flops 399360 | bytes 491620 | tf_op jit(solution)/shard_map/reduce_sum | solution.py:73
  231.1 0.2 copy.79
  231.3 5.8 %fusion.16 = f32[128,8,10]{1,2,0:T(8,128)S(1)} fusion(f32[128,10,8,64]{3,2,1,0:T(8,128)} %get-tuple-element.16, f32[128,8,10]{1,2,0:T(8,128)S(1)} %copy.76), kind=kLoop, calls=%fused_computation.29 | loop fusion | flops 1955840 | bytes 2703360 | tf_op jit(solution)/shard_map/reduce_sum | solution.py:73
  237.2 0.3 copy.78
  237.5 0.5 copy.80
  238.0 0.3 copy.83
  238.2 1.1 slice.61
  239.3 7.3 %fusion.42 = bf16[128,8,10,64]{3,1,2,0:T(8,128)(2,1)} fusion(f32[128,8,10]{1,2,0:T(8,128)S(1)} %copy.80, f32[128,8,10]{1,2,0:T(8,128)S(1)} %copy.76, f32[128,10,8,64]{3,2,1,0:T(8,128)} %get-tuple-element.16), kind=kLoop, calls=%fused_computation.49 | loop fusion | flops 2621440 | bytes 4014080 | tf_op jit(solution)/shard_map/reshape.10
  246.7 0.1 reshape.282
  246.8 7.2 %fusion.18 = f32[128,128,8,10]{1,3,2,0:T(8,128)} fusion(f32[128,10,10,8]{2,1,3,0:T(8,128)} %get-tuple-element.18, f32[128,8,10]{2,1,0:T(8,128)S(1)} %copy.83, f32[128,8,10]{2,1,0:T(8,128)S(1)} %copy.77, pred[10,10]{0,1:T(8,128)(4,1)S(1)} %iota_compare_fusion, bf16[128,10,128,1]{2,1,0,3:T(8,128)(2,1)S(1)} %reshape.282), kind=kOutput, calls=%fused_computation.31 | convolution fusion | flops 26726400 | bytes 6062180 | tf_op jit(solution)/shard_map/skgtu,sukd->stkgd/dot_general | solution.py:79
  254.1 4.8 %fusion.17 = bf16[128,10,1,8,128]{4,1,3,0,2:T(8,128)(2,1)S(1)} fusion(f32[128,128,8,10]{1,3,2,0:T(8,128)} %fusion.18, bf16[128,8,10,64]{3,1,2,0:T(8,128)(2,1)S(1)} %copy-done.3, bf16[128,64,1,128]{3,2,1,0:T(2,128)(2,1)S(1)} %copy-done.4), kind=kOutput, calls=%fused_computation.30 | convolution fusion | flops 170393600 | bytes 11272192 | tf_op jit(solution)/shard_map/skgtc,sckd->stkgd/dot_general | solution.py:76
  258.9 2.9 copy.85
  261.9 5.2 %reshape.283 = bf16[1280,1024,1]{1,0,2:T(8,128)(2,1)} reshape(bf16[128,10,1,8,128]{4,3,1,0,2:T(8,128)(2,1)} %copy.85) | data formatting | bytes 5242880 | tf_op jit(solution)/shard_map/convert_element_type | solution.py:82
  267.0 16.1 %fusion.1 = bf16[1280,32,128]{2,0,1:T(8,128)(2,1)} fusion(bf16[1280,1024,1]{1,0,2:T(8,128)(2,1)} %reshape.283, bf16[32,128,1024]{2,1,0:T(8,128)(2,1)} %bitcast.114, f32[1280,32]{0,1:T(8,128)S(1)} %copy-done.8), kind=kOutput, calls=%fused_computation.2 | convolution fusion | flops 10753146880 | bytes 21659648 | tf_op jit(solution)/shard_map/dot_general | solution.py:114
  283.1 14.4 %copy.87 = bf16[1280,32,128]{0,2,1:T(8,128)(2,1)} copy(bf16[1280,32,128]{2,0,1:T(8,128)(2,1)} %fusion.1) | data formatting | bytes 20971520 | tf_op jit(solution)/shard_map/optimization_barrier | solution.py:119
  297.5 14.3 %copy.96 = bf16[1280,4096]{1,0:T(8,128)(2,1)} copy(bf16[1280,4096]{0,1:T(8,128)(2,1)} %bitcast.107) | data formatting | bytes 20971520
  311.8 0.0 reduce-scatter.4.cloned.1.call-update
  311.9 0.0 copy-start.1
  311.9 1.0 multiply_exponential_fusion.1
  312.9 0.1 copy.89
  313.0 110.4 %reduce-scatter.4.cloned.1.call-done = bf16[160,4096]{1,0:T(8,128)(2,1)} async-done(((bf16[1280,4096]{1,0:T(8,128)(2,1)}), bf16[160,4096]{1,0:T(8,128)(2,1)}) %reduce-scatter.4.cloned.1.call-update) | async-done | bytes 1310736 | tf_op jit(solution)/shard_map/reduce_scatter | solution.py:122
  423.4 0.7 mul.287
  424.1 4.3 fusion.41
  (35 shorter events, 0.2 us)
Async XLA Ops:
  6.5 150.1 %copy-start = (bf16[4096,128]{1,0:T(8,128)(2,1)S(1)}, bf16[4096,128]{1,0:T(8,128)(2,1)}, u32[]{:S(2)}) copy-start(bf16[4096,128]{1,0:T(8,128)(2,1)} %param.12) | copy-start | bytes 3145732
  6.5 68.1 %all-gather.5.cloned.1.call-start = ((), (), s32[]{:S(2)}) async-start(), calls=%async_computation.1 | async-start | bytes 5898240 | tf_op jit(solution)/shard_map/all_gather | solution.py:28
  9.1 128.4 %all-gather.7.cloned.1.call-start = ((), (), s32[]{:S(2)}) async-start(), calls=%async_computation.2 | async-start | bytes 5898240 | tf_op jit(solution)/shard_map/all_gather | solution.py:28
  9.9 413.5 %reduce-scatter.4.cloned.1.call-start = ((), (), s32[]{:S(2)}) async-start(), calls=%async_computation.3 | async-start | bytes 11796480 | tf_op jit(solution)/shard_map/reduce_scatter | solution.py:122
  10.6 12.1 %copy-start.7 = (s32[1280,32]{0,1:T(8,128)S(1)}, s32[1280,32]{0,1:T(8,128)}, u32[]{:S(2)}) copy-start(s32[1280,32]{0,1:T(8,128)} %param.15) | copy-start | bytes 491524
  137.5 4.0 copy-start.5
  137.5 13.5 %slice-start = ((s8[5242880]{0:T(1024)(128)(4,1)}), s8[4194304]{0:T(1024)(128)(4,1)S(1)}, s32[]{:S(2)}) async-start(s8[5242880]{0:T(1024)(128)(4,1)} %bitcast.120), calls=%async_computation.4 | async-start | bytes 8388608
  137.5 13.5 %slice-start.2 = ((s8[8388608]{0:T(1024)(128)(4,1)}), s8[4194304]{0:T(1024)(128)(4,1)S(1)}, s32[]{:S(2)}) async-start(s8[8388608]{0:T(1024)(128)(4,1)} %bitcast.126), calls=%async_computation.6 | async-start | bytes 8388608
  141.5 9.4 %slice-start.1 = ((s8[5242880]{0:T(1024)(128)(4,1)}), s8[1048576]{0:T(1024)(128)(4,1)S(1)}, s32[]{:S(2)}) async-start(s8[5242880]{0:T(1024)(128)(4,1)} %bitcast.120), calls=%async_computation.5 | async-start | bytes 2097152
  141.5 9.4 %slice-start.3 = ((s8[8388608]{0:T(1024)(128)(4,1)}), s8[4194304]{0:T(1024)(128)(4,1)S(1)}, s32[]{:S(2)}) async-start(s8[8388608]{0:T(1024)(128)(4,1)} %bitcast.126), calls=%async_computation.7 | async-start | bytes 8388608
  158.3 1.6 copy-start.9
  163.7 4.4 %copy-start.2 = (f32[8,160,1280]{2,1,0:T(8,128)}, f32[8,160,1280]{2,1,0:T(8,128)S(1)}, u32[]{:S(2)}) copy-start(f32[8,160,1280]{2,1,0:T(8,128)S(1)} %maximum_maximum_fusion) | copy-start | bytes 19660804
  246.8 7.2 %copy-start.3 = (bf16[128,8,10,64]{3,1,2,0:T(8,128)(2,1)S(1)}, bf16[128,8,10,64]{3,1,2,0:T(8,128)(2,1)}, u32[]{:S(2)}) copy-start(bf16[128,8,10,64]{3,1,2,0:T(8,128)(2,1)} %fusion.42) | copy-start | bytes 3932164
  246.8 7.2 %copy-start.4 = (bf16[128,64,1,128]{3,2,1,0:T(2,128)(2,1)S(1)}, bf16[128,64,1,128]{3,2,1,0:T(2,128)(2,1)}, u32[]{:S(2)}) copy-start(bf16[128,64,1,128]{3,2,1,0:T(2,128)(2,1)} %get-tuple-element.7) | copy-start | bytes 6291460
  258.9 8.1 %copy-start.8 = (f32[1280,32]{0,1:T(8,128)S(1)}, f32[1280,32]{0,1:T(8,128)}, u32[]{:S(2)}) copy-start(f32[1280,32]{0,1:T(8,128)} %multiply_exponential_fusion) | copy-start | bytes 491524
  311.8 112.3 %copy-start.6 = (bf16[160,4096]{1,0:T(8,128)(2,1)S(1)}, bf16[160,4096]{1,0:T(8,128)(2,1)}, u32[]{:S(2)}) copy-start(bf16[160,4096]{1,0:T(8,128)(2,1)} %param.8) | copy-start | bytes 3932164
  311.9 116.6 %copy-start.1 = (bf16[4096,128]{1,0:T(8,128)(2,1)S(1)}, bf16[4096,128]{1,0:T(8,128)(2,1)}, u32[]{:S(2)}) copy-start(bf16[4096,128]{1,0:T(8,128)(2,1)} %param.12) | copy-start | bytes 3145732
Sparse Core Ops, SparseCore 0:
  9.2 65.3 all-gather.4
  76.3 61.1 all-gather.6
  312.0 111.3 reduce-scatter.3
where the time goes:
time: 443 us; the launch traced here: 435 us
  waiting for transfers between devices  205 us (46%)
  local copies, waits for them, and re-layouts  104 us (23%)
  matrix products  71.4 us (16%)
  other arithmetic  41 us (9%)
  between operations  13.7 us (3%)
    reduce_scatter x1, waiting for transfers between devices, on_device(): lax.psum_scatter(rounded.astype(jnp.bfloat16), 'tensor', scatter_dimensio...  110 us
    all_gather x2, waiting for transfers between devices, work_in_pieces(): finished.append(jax.vmap(apply)(lax.all_gather(share, axis), starts))  93.7 us
    unnamed x31, local copies, waits for them, and re-layouts  21.8 us
    dot_general x1, matrix products, on_device(): jnp.dot(attended, out_weight, preferred_element_type=jnp.float32)  16.1 us
    slice x1, local copies, waits for them, and re-layouts, attention(): past_cache[:, :, 1].reshape(seq_count, cache_len, kv_heads, HD)  15.5 us
    dot_general x2, matrix products, project(): jnp.dot(normed, query_weight, preferred_element_type=jnp.float32)  15.1 us
    dot_general x1, matrix products, attention(): jnp.einsum('stkgd,sukd->skgtu', query_heads, new_keys, preferred_element_...  15 us
    optimization_barrier x1, local copies, waits for them, and re-layouts, on_device(): lax.optimization_barrier(scaled.astype(jnp.bfloat16)).astype(jnp.float32)  14.4 us
  transfers between devices with their start and end apart: 3, of which 3 were waited for; matrix products, arithmetic and copies ran while one was open for 8% of the time, Pallas kernels for 0%

commit v1 on v0

v1 whole, which is shorter than its diff:
```python
import jax
import jax.numpy as jnp
import numpy as np
from jax import lax
from jax.experimental import pallas as pl
from jax.experimental.pallas import tpu as pltpu
from jax.sharding import PartitionSpec as P


HD = 128
NEW = 10
CACHE = 64
HEADS = 8
PAD = 16
BLOCK = 80
CHUNK = 16
LIMIT = 20 << 20
epsilon = 1e-05
theta_base = 500000.0


VMEM = pltpu.VMEM


def hbm(x):
    return pltpu.with_memory_space_constraint(x, pltpu.HBM)


def vmem(x):
    return pltpu.with_memory_space_constraint(x, VMEM)


def norm_kernel(first, tokens, gain, out, x, g, sems):
    rows, width = out.shape
    gain_copy = pltpu.make_async_copy(gain, g, sems.at[rows // CHUNK])
    gain_copy.start()
    for i in range(rows // CHUNK):
        pltpu.make_async_copy(
            tokens.at[pl.ds(first + i * CHUNK, CHUNK)], x.at[pl.ds(i * CHUNK, CHUNK)], sems.at[i]
        ).start()
    gain_copy.wait()

    @pl.loop(0, rows // CHUNK)
    def _(i):
        span = pl.ds(pl.multiple_of(i * CHUNK, CHUNK), CHUNK)
        pltpu.make_async_copy(x.at[span], x.at[span], sems.at[i]).wait()
        floats = x[span, :].astype(jnp.float32)
        scale = lax.rsqrt(jnp.mean(floats * floats, axis=-1, keepdims=True) + epsilon)
        for c in range(width // HD):
            cols = slice(c * HD, (c + 1) * HD)
            part = x[span, cols].astype(jnp.float32) * scale * g[c : c + 1].astype(jnp.float32)
            out[span, cols] = part.astype(jnp.bfloat16)


def norm_half(tokens, gain, half):
    rows, width = tokens.shape[0] // 2, tokens.shape[1]
    anywhere = pl.BlockSpec(memory_space=pl.ANY)
    return pl.pallas_call(
        lambda *refs: norm_kernel(half * rows, *refs),
        in_specs=[anywhere] * 2,
        out_specs=pl.BlockSpec(memory_space=VMEM),
        out_shape=VMEM((rows, width), jnp.bfloat16),
        scratch_shapes=[
            VMEM((rows, width), jnp.bfloat16),
            VMEM((width // HD, HD), jnp.bfloat16),
            pltpu.SemaphoreType.DMA((rows // CHUNK + 1,)),
        ],
        compiler_params=pltpu.CompilerParams(vmem_limit_bytes=LIMIT),
    )(hbm(tokens), hbm(gain))


def rotary_tables(rows):
    half = HD // 2
    positions = (np.arange(rows) % NEW + CACHE).astype(np.float32)
    frequency = np.float32(theta_base) ** (-(np.arange(half, dtype=np.float32) * 2.0) / HD)
    angles = positions[:, None] * frequency[None, :].astype(np.float32)
    cosine = np.cos(angles).astype(np.float32)
    sine = np.sin(angles).astype(np.float32)
    return np.concatenate([cosine, cosine], 1), np.concatenate([-sine, sine], 1)


def pad_matrix(rows):
    seqs = rows // NEW
    matrix = np.zeros((seqs * PAD, rows), np.float32)
    for s in range(seqs):
        for t in range(NEW):
            matrix[s * PAD + t, s * NEW + t] = 1.0
    return matrix


def odd_matrix(rows):
    seqs = rows // NEW
    matrix = np.zeros((seqs * 2 * CACHE, rows), np.float32)
    for s in range(seqs):
        for u in range(NEW):
            matrix[s * 2 * CACHE + 2 * u + 1, s * NEW + u] = 1.0
    return matrix


def powers(exponent, sign):
    total = jnp.zeros(exponent.shape, jnp.float32)
    for e in range(7, 12):
        total = jnp.where(exponent == -e, 2.0 ** (sign * e), total)
    return total


def spread_matrix(groups, per_slab):
    matrix = np.zeros((groups // per_slab, groups, per_slab * HD), np.float32)
    for g in range(groups):
        matrix[g // per_slab, g, (g % per_slab) * HD : (g % per_slab + 1) * HD] = 1.0
    return matrix


def block_kernel(spots, sizes, *refs):
    count, blocks = len(sizes), len(spots)
    (offsets, *refs) = refs
    pieces, refs = refs[:count], refs[count:]
    (qw, kw, vw, ow, cache, exps, cos, sin, pad, unpad, odd, spread, *refs) = refs
    outs, refs = refs[:count], refs[count:]
    (kv, ex, qs, kvs, qp, op, fresh, scores, probs, att, sems) = refs
    slab, out_slab = 256, 1024
    slabs, out_slabs = qw.shape[1] // slab, ow.shape[1] // out_slab
    seqs = BLOCK // NEW
    kv_rows = seqs * 2 * CACHE
    starts = [sum(sizes[:p]) for p in range(count)]

    copies = []
    for b, (owner, first) in enumerate(spots):
        first = pl.multiple_of(offsets[owner] + first, 8)
        cache_first = pl.multiple_of(first // NEW * (2 * CACHE), 8)
        for source, target in (
            (cache.at[pl.ds(cache_first, kv_rows)], kv.at[pl.ds(b * kv_rows, kv_rows)]),
            (exps.at[pl.ds(first, BLOCK)], ex.at[pl.ds(b * BLOCK, BLOCK)]),
        ):
            copy = pltpu.make_async_copy(source, target, sems.at[len(copies)])
            copy.start()
            copies.append(copy)

    cosine = jnp.concatenate([cos[...]] * blocks, 0)
    sine = jnp.concatenate([sin[...]] * blocks, 0)

    def rotate(m):
        swapped = pltpu.roll(m, HD // 2, 1)
        return (m * cosine + swapped * sine).astype(jnp.bfloat16)

    def rows():
        return jnp.concatenate([piece[...] for piece in pieces], 0)

    y = jnp.dot(
        rows(), jnp.concatenate([kw[...], vw[...]], 1), preferred_element_type=jnp.float32
    )
    kvs[:, :HD] = rotate(y[:, :HD])
    kvs[:, HD:] = y[:, HD:].astype(jnp.bfloat16)

    @pl.loop(0, slabs)
    def _(i):
        cols = pl.ds(pl.multiple_of(i * slab, slab), slab)
        y = jnp.dot(rows(), qw[:, cols], preferred_element_type=jnp.float32)
        for h in range(slab // HD):
            qs[i, :, h * HD : (h + 1) * HD] = rotate(y[:, h * HD : (h + 1) * HD])

    for copy in copies:
        copy.wait()
    tall = HEADS * PAD
    inv_root = 1.0 / HD**0.5
    contract_last = (((1,), (1,)), ((), ()))
    lane = lax.broadcasted_iota(jnp.int32, (tall, 2 * CACHE), 1)
    step = lax.broadcasted_iota(jnp.int32, (tall, 2 * CACHE), 0) % PAD
    is_old = lane % 2 == 0
    allowed = is_old | ((lane // 2 <= step) & (lane // 2 < NEW))

    @pl.loop(0, blocks)
    def _(b):
        own = pl.ds(pl.multiple_of(b * BLOCK, BLOCK), BLOCK)
        for i in range(slabs):
            qp[i] = jnp.dot(pad[...], qs[i, own, :], preferred_element_type=jnp.float32).astype(
                jnp.bfloat16
            )
        fresh[...] = jnp.dot(odd[...], kvs[own, :], preferred_element_type=jnp.float32).astype(
            jnp.bfloat16
        )

        def pairs(s):
            first = pl.multiple_of(b * kv_rows + s * 2 * CACHE, 2 * CACHE)
            return kv[pl.ds(first, 2 * CACHE), :]

        def fresh_span(s):
            return slice(s * 2 * CACHE, (s + 1) * 2 * CACHE)

        per = slab // HD
        for s in range(seqs):
            base = s * PAD
            query = jnp.concatenate(
                [
                    qp[h // per, base : base + PAD, h % per * HD : (h % per + 1) * HD]
                    for h in range(HEADS)
                ],
                0,
            )
            span = slice(s * tall, (s + 1) * tall)
            keys = jnp.concatenate([pairs(s), fresh[fresh_span(s), :HD]], 0)
            both = lax.dot_general(query, keys, contract_last, preferred_element_type=jnp.float32)
            score = jnp.where(is_old, both[:, : 2 * CACHE], both[:, 2 * CACHE :]) * inv_root
            scores[span] = jnp.where(allowed, score, -1e30)
        for s in range(seqs):
            span = slice(s * tall, (s + 1) * tall)
            score = scores[span]
            prob = jnp.exp(score - jnp.max(score, axis=-1, keepdims=True))
            prob = prob / jnp.sum(prob, axis=-1, keepdims=True)
            rolled = jnp.where(is_old, 0.0, pltpu.roll(prob, 1, 1))
            probs[span, : 2 * CACHE] = rolled.astype(jnp.bfloat16)
            probs[span, 2 * CACHE :] = prob.astype(jnp.bfloat16)
        for s in range(seqs):
            base = s * PAD
            span = slice(s * tall, (s + 1) * tall)
            values = jnp.concatenate([pairs(s), fresh[fresh_span(s), HD:]], 0)
            got = jnp.dot(probs[span], values, preferred_element_type=jnp.float32)
            got = got.astype(jnp.bfloat16)
            for h in range(HEADS):
                op[base : base + PAD, h * HD : (h + 1) * HD] = got[h * PAD : (h + 1) * PAD]
        att[own, :] = jnp.dot(unpad[...], op[...], preferred_element_type=jnp.float32).astype(
            jnp.bfloat16
        )

    shrinks = powers(ex[...], 1).astype(jnp.bfloat16)

    @pl.loop(0, out_slabs)
    def _(i):
        cols = pl.ds(pl.multiple_of(i * out_slab, out_slab), out_slab)
        y = jnp.dot(att[...], ow[:, cols], preferred_element_type=jnp.float32)
        shrink = jnp.dot(shrinks, spread[i], preferred_element_type=jnp.float32)
        scaled = jnp.clip(y * shrink, -127.0, 127.0).astype(jnp.bfloat16)
        for p in range(count):
            outs[p][:, cols] = scaled[starts[p] : starts[p] + sizes[p]]


def block(offsets, spots, pieces, weights):
    width = pieces[0].shape[1]
    sizes = [piece.shape[0] for piece in pieces]
    count, total = len(pieces), sum(sizes)
    seqs = BLOCK // NEW
    head_cols = HEADS * HD
    slab, out_slab = 256, 1024
    cos, sin = rotary_tables(BLOCK)
    pad = pad_matrix(BLOCK)
    spread = spread_matrix(width // HD, out_slab // HD)
    smem = pl.BlockSpec(memory_space=pltpu.SMEM)
    anywhere = pl.BlockSpec(memory_space=pl.ANY)
    inside = pl.BlockSpec(memory_space=VMEM)
    flops = 2 * total * width * (head_cols + 2 * HD) + 2 * total * head_cols * width
    call = pl.pallas_call(
        lambda *refs: block_kernel(spots, sizes, *refs),
        in_specs=[smem] + [inside] * (count + 4) + [anywhere] * 2 + [inside] * 6,
        out_specs=[inside] * count,
        out_shape=[VMEM((rows, width), jnp.bfloat16) for rows in sizes],
        scratch_shapes=[
            VMEM((len(spots) * seqs * 2 * CACHE, HD), jnp.bfloat16),
            VMEM((total, width // HD), jnp.int32),
            VMEM((head_cols // slab, total, slab), jnp.bfloat16),
            VMEM((total, 2 * HD), jnp.bfloat16),
            VMEM((head_cols // slab, seqs * PAD, slab), jnp.bfloat16),
            VMEM((seqs * PAD, head_cols), jnp.bfloat16),
            VMEM((seqs * 2 * CACHE, 2 * HD), jnp.bfloat16),
            VMEM((seqs * HEADS * PAD, 2 * CACHE), jnp.float32),
            VMEM((seqs * HEADS * PAD, 4 * CACHE), jnp.bfloat16),
            VMEM((total, head_cols), jnp.bfloat16),
            pltpu.SemaphoreType.DMA((2 * len(spots),)),
        ],
        compiler_params=pltpu.CompilerParams(vmem_limit_bytes=LIMIT),
        cost_estimate=pl.CostEstimate(flops=flops, transcendentals=0, bytes_accessed=20 << 20),
    )
    return call(
        offsets,
        *[vmem(piece) for piece in pieces],
        *weights,
        jnp.asarray(cos),
        jnp.asarray(sin),
        jnp.asarray(pad, jnp.bfloat16),
        jnp.asarray(pad.T, jnp.bfloat16),
        jnp.asarray(odd_matrix(BLOCK), jnp.bfloat16),
        jnp.asarray(spread, jnp.bfloat16),
    )


def add_kernel(jobs, *refs):
    count = len(jobs)
    bases, parts, outs = refs[:count], list(refs[count:-count]), refs[-count:]
    for base, out, (first, rows, n) in zip(bases, outs, jobs):
        mine, parts = parts[:n], parts[n:]

        @pl.loop(0, rows // CHUNK)
        def _(i, base=base, out=out, first=first, mine=mine):
            here = pl.ds(pl.multiple_of(first + i * CHUNK, CHUNK), CHUNK)
            span = pl.ds(pl.multiple_of(i * CHUNK, CHUNK), CHUNK)
            total = base[here, :].astype(jnp.float32)
            for part in mine:
                total = total + part[span, :].astype(jnp.float32)
            out[here, :] = total.astype(jnp.bfloat16)


def add_rows(*jobs):
    bases = [base for base, _, _ in jobs]
    parts = [part for _, _, some in jobs for part in some]
    shapes = [(first, some[0].shape[0], len(some)) for _, first, some in jobs]
    rows, width = max(r for _, r, _ in shapes), bases[0].shape[1]
    inside = pl.BlockSpec(memory_space=VMEM)
    return pl.pallas_call(
        lambda *refs: add_kernel(shapes, *refs),
        in_specs=[inside] * (len(bases) + len(parts)),
        out_specs=[inside] * len(bases),
        out_shape=[VMEM(base.shape, jnp.bfloat16) for base in bases],
        input_output_aliases={j: j for j in range(len(bases))},
        compiler_params=pltpu.CompilerParams(vmem_limit_bytes=LIMIT),
        cost_estimate=pl.CostEstimate(
            flops=rows * width * 64 * len(bases), transcendentals=0, bytes_accessed=rows * width * 6
        ),
    )(*[vmem(x) for x in (*bases, *parts)])


def final_kernel(half, tokens, exps, *refs):
    (*parts, out, x, exponent, e, y, sems, out_sems) = refs
    parts = parts[:4]
    rows, width = parts[0].shape
    chunks = rows // CHUNK
    first = half * rows
    e_copy = pltpu.make_async_copy(exps.at[pl.ds(first, rows)], exponent, sems.at[chunks])
    e_copy.start()
    for i in range(chunks):
        pltpu.make_async_copy(
            tokens.at[pl.ds(first + i * CHUNK, CHUNK)], x.at[pl.ds(i * CHUNK, CHUNK)], sems.at[i]
        ).start()
    e_copy.wait()
    e[...] = powers(exponent[...], -1)

    def out_copy(i):
        return pltpu.make_async_copy(
            y.at[pl.ds(i * CHUNK, CHUNK)],
            out.at[pl.ds(first + i * CHUNK, CHUNK)],
            out_sems.at[i],
        )

    @pl.loop(0, chunks)
    def _(i):
        span = pl.ds(pl.multiple_of(i * CHUNK, CHUNK), CHUNK)
        pltpu.make_async_copy(x.at[span], x.at[span], sems.at[i]).wait()
        restore = e[span, :]
        for g in range(width // HD):
            cols = slice(g * HD, (g + 1) * HD)
            summed = parts[0][span, cols].astype(jnp.float32)
            for part in parts[1:]:
                summed = summed + part[span, cols].astype(jnp.float32)
            mixed = x[span, cols].astype(jnp.float32) + summed * restore[:, g : g + 1]
            y[span, cols] = mixed.astype(jnp.bfloat16)
        out_copy(i).start()

    for i in range(chunks):
        out_copy(i).wait()


def final_half(tokens, exps, parts, half, previous=None):
    rows, width = parts[0].shape
    anywhere = pl.BlockSpec(memory_space=pl.ANY)
    inputs = [hbm(tokens), hbm(exps), *[vmem(part) for part in parts]]
    specs = [anywhere] * 2 + [pl.BlockSpec(memory_space=VMEM)] * len(parts)
    aliases = {}
    if previous is not None:
        inputs.append(previous)
        specs.append(anywhere)
        aliases = {len(inputs) - 1: 0}
    return pl.pallas_call(
        lambda *refs: final_kernel(half, *refs),
        in_specs=specs,
        out_specs=anywhere,
        out_shape=pltpu.HBM(tokens.shape, jnp.bfloat16),
        input_output_aliases=aliases,
        scratch_shapes=[
            VMEM((rows, width), jnp.bfloat16),
            VMEM((rows, exps.shape[1]), jnp.int32),
            VMEM((rows, exps.shape[1]), jnp.float32),
            VMEM((rows, width), jnp.bfloat16),
            pltpu.SemaphoreType.DMA((rows // CHUNK + 1,)),
            pltpu.SemaphoreType.DMA((rows // CHUNK,)),
        ],
        compiler_params=pltpu.CompilerParams(vmem_limit_bytes=LIMIT),
        cost_estimate=pl.CostEstimate(
            flops=rows * width * 64, transcendentals=0, bytes_accessed=rows * width * 12
        ),
    )(*inputs)


OWN, A, B, C, U, V, W, Z = range(8)


def solution(mesh):
    ring = 4
    pairs = mesh.shape["tensor"] // ring
    assert pairs == 2
    cells = [(x, y) for x in range(pairs) for y in range(ring)]
    up = [(x * ring + y, x * ring + (y + 1) % ring) for x, y in cells]
    down = [(x * ring + y, x * ring + (y - 1) % ring) for x, y in cells]
    across = [(x * ring + y, (1 - x) * ring + y) for x, y in cells]

    def owners(x, y):
        steps = ((0, 0), (0, -1), (0, 1), (1, 0), (1, -1), (1, 1), (0, 2), (1, 2))
        return [(x + dx) % pairs * ring + (y + dy) % ring for dx, dy in steps]

    table = np.array([owners(x, y) for x, y in cells], np.int32)

    def move(value, where):
        return lax.ppermute(value, "tensor", where)

    def on_device(
        tokens, norm_gain, query_weight, key_weight, value_weight, out_weight, past_cache, exponents
    ):
        own_rows = tokens.shape[0]
        half = own_rows // 2
        cut0, cut1 = 3 * CHUNK, 2 * CHUNK
        index = lax.axis_index("tensor")
        offsets = lax.dynamic_index_in_dim(jnp.asarray(table * own_rows), index, 0, False)

        seqs, cached = past_cache.shape[:2]
        cache = past_cache.reshape(seqs * cached * 2, HD)
        resident = [
            vmem(weight) for weight in (query_weight, key_weight, value_weight, out_weight)
        ]
        weights = (*resident, hbm(cache), hbm(exponents))
        gain = norm_gain.reshape(-1, HD)
        own_exponents = lax.dynamic_slice_in_dim(exponents, index * own_rows, own_rows, 0)

        n0 = norm_half(tokens, gain, 0)
        a0, b0, c0 = move(n0, up), move(n0, down), move(n0, across)
        n1 = norm_half(tokens, gain, 1)
        a1, b1, c1 = move(n1, up), move(n1, down), move(n1, across)
        u0, w0, v0 = move(a0, across), move(a0, up), move(c0, down)
        v1, u1, w1 = move(b1, across), move(c1, up), move(b1, down)
        z0a, z0b = move(u0[:cut0], up), move(v0[cut0:], down)
        z1a, z1b = move(u1[:cut1], up), move(v1[cut1:], down)

        near, far = (A, B, C), (U, V, W)
        own0, own1 = block(offsets, [(OWN, 0), (OWN, half)], [n0, n1], weights)

        def spots(which, start):
            return [(w, start) for w in which]

        pa0, pb0, pc0 = block(offsets, spots(near, 0), [a0, b0, c0], weights)
        pa1, pb1, pc1 = block(offsets, spots(near, half), [a1, b1, c1], weights)
        pu0, pv0, pw0 = block(offsets, spots(far, 0), [u0, v0, w0], weights)
        pu1, pv1, pw1 = block(offsets, spots(far, half), [u1, v1, w1], weights)
        pz0a, pz0b = block(offsets, [(Z, 0)], [z0a, z0b], weights)
        pz1a, pz1b = block(offsets, [(Z, half)], [z1a, z1b], weights)

        ru0, rv0 = move(pz0a, down), move(pz0b, up)
        ru1, rv1 = move(pz1a, down), move(pz1b, up)
        pu0, pv0 = add_rows((pu0, 0, [ru0]), (pv0, cut0, [rv0]))
        fu0, fw0, fv0 = move(pu0, across), move(pw0, down), move(pv0, up)
        pu1, pv1 = add_rows((pu1, 0, [ru1]), (pv1, cut1, [rv1]))
        fv1, fu1, fw1 = move(pv1, across), move(pu1, down), move(pw1, up)
        pa0, pc0 = add_rows((pa0, 0, [fu0, fw0]), (pc0, 0, [fv0]))
        ga0, gb0, gc0 = move(pa0, down), move(pb0, up), move(pc0, across)
        pb1, pc1 = add_rows((pb1, 0, [fv1, fw1]), (pc1, 0, [fu1]))
        ga1, gb1, gc1 = move(pa1, down), move(pb1, up), move(pc1, across)
        out = final_half(tokens, own_exponents, [own0, ga0, gb0, gc0], 0)
        return final_half(tokens, own_exponents, [own1, ga1, gb1, gc1], 1, out)

    return jax.shard_map(
        on_device,
        mesh=mesh,
        in_specs=(
            P(("dp", "tensor"), None),
            P(),
            P(None, "tensor"),
            P(None, "tensor"),
            P(None, "tensor"),
            P("tensor", None),
            P("dp", None, None, "tensor"),
            P("dp", None),
        ),
        out_specs=P(("dp", "tensor"), None),
        check_vma=False,
    )
```

time: 443 us -> 215 us (0.49)
  the two profiles are of different devices: /device:TPU:1 before, /device:TPU:0 now
where the time goes in v1:
time: 215 us
  Pallas kernels  101 us (47%)
  waiting for transfers between devices  43.7 us (20%)
  starting transfers between devices  43.3 us (20%)
  local copies, waits for them, and re-layouts  26.3 us (12%)
    pallas_call x7, Pallas kernels, block(): call(offsets, *[vmem(piece) for piece in pieces], *weights, jnp.asarray(c...  83.2 us
    ppermute x32, waiting for transfers between devices, move(): return lax.ppermute(value, 'tensor', where)  43.7 us
    ppermute x32, starting transfers between devices, move(): return lax.ppermute(value, 'tensor', where)  43.3 us
    unnamed x67, local copies, waits for them, and re-layouts  20.9 us
    pallas_call x2, Pallas kernels, final_half(): pl.pallas_call(lambda *refs: final_kernel(half, *refs), in_specs=specs, o...  7.89 us
    pallas_call x4, Pallas kernels, add_rows(): pl.pallas_call(lambda *refs: add_kernel(shapes, *refs), in_specs=[inside]...  5.93 us
  transfers between devices with their start and end apart: 32, of which 5 were waited for; matrix products, arithmetic and copies ran while one was open for 3% of the time, Pallas kernels for 44%

profile of v1, /device:TPU:0, one launch (start us, length us, event | category | flops | bytes accessed | tf_op | source)
XLA Modules:
  0.0 214.6 jit_solution(10145858271218092376)
XLA Ops:
  0.0 1.9 shard_map.469.refs_1_
  2.0 1.8 collective-permute-start.16
  3.7 1.5 collective-permute-start.18
  5.2 1.8 shard_map.470.refs_2_
  7.0 1.7 collective-permute-start.1
  8.7 0.4 collective-permute-start.2
  9.2 10.9 %collective-permute-done.16.refs_1_ = bf16[80,4096]{1,0:T(8,128)(2,1)} collective-permute-done((bf16[80,4096]{1,0:T(8,128)(2,1)S(1)}, bf16[80,4096]{1,0:T(8,128)(2,1)}, u32[]{:S(2)}, u32[]{:S(2)}) %collective-permute-start.16) | collective-permute-done | bytes 655392 | tf_op jit(solution)/shard_map/ppermute | solution.py:410
  20.0 1.5 collective-permute-start.19
  21.5 1.7 collective-permute-start.20
  23.3 0.8 copy-done.27
  24.1 1.2 collective-permute-start.5
  25.3 10.0 %collective-permute-done.2.refs_3_ = bf16[80,4096]{1,0:T(8,128)(2,1)S(1)} collective-permute-done((bf16[80,4096]{1,0:T(8,128)(2,1)S(1)}, bf16[80,4096]{1,0:T(8,128)(2,1)S(1)}, u32[]{:S(2)}, u32[]{:S(2)}) %collective-permute-start.2) | collective-permute-done | bytes 655392 | tf_op jit(solution)/shard_map/ppermute | solution.py:410
  35.4 1.6 collective-permute-start.4
  37.0 0.8 copy-done.25
  37.8 11.6 %collective-permute-done.19.refs_1_ = bf16[80,4096]{1,0:T(8,128)(2,1)S(1)} collective-permute-done((bf16[80,4096]{1,0:T(8,128)(2,1)}, bf16[80,4096]{1,0:T(8,128)(2,1)S(1)}, u32[]{:S(2)}, u32[]{:S(2)}) %collective-permute-start.19) | collective-permute-done | bytes 655392 | tf_op jit(solution)/shard_map/ppermute | solution.py:410
  49.4 0.8 slice.18
  50.3 1.6 collective-permute-start.22
  51.9 1.3 collective-permute-start.21
  53.2 0.8 slice.19
  53.9 2.0 collective-permute-start.23
  55.9 6.2 %collective-permute-done.5.refs_2_ = bf16[80,4096]{1,0:T(8,128)(2,1)S(1)} collective-permute-done((bf16[80,4096]{1,0:T(8,128)(2,1)S(1)}, bf16[80,4096]{1,0:T(8,128)(2,1)S(1)}, u32[]{:S(2)}, u32[]{:S(2)}) %collective-permute-start.5) | collective-permute-done | bytes 655392 | tf_op jit(solution)/shard_map/ppermute | solution.py:410
  62.1 0.8 slice.17
  62.9 0.8 copy-done.13
  63.7 1.8 collective-permute-start.8
  65.5 0.7 slice.16
  66.2 0.8 copy-done.18
  67.1 0.2 collective-permute-start.7
  67.3 2.0 copy.61.refs_8_.refs_9_
  69.3 0.7 dynamic-slice_bitcast_fusion.refs_0_
  70.0 3.0 %collective-permute-start.17 = (bf16[80,4096]{1,0:T(8,128)(2,1)S(1)}, bf16[80,4096]{1,0:T(8,128)(2,1)S(1)}, u32[]{:S(2)}, u32[]{:S(2)}) collective-permute-start(bf16[80,4096]{1,0:T(8,128)(2,1)S(1)} %shard_map.469.refs_1_), channel_id=1, source_target_pairs={{0,3},{1,0},{2,1},{3,2},{4,7},{5,4},{6,5},{7,6},{8,11},{9,8},{10,9... | collective-permute-start | bytes 1966088 | tf_op jit(solution)/shard_map/ppermute | solution.py:410
  73.0 0.4 collective-permute-start.6
  73.5 3.4 %copy-done = bf16[4096,1024]{1,0:T(8,128)(2,1)S(1)} copy-done((bf16[4096,1024]{1,0:T(8,128)(2,1)S(1)}, bf16[4096,1024]{1,0:T(8,128)(2,1)}, u32[]{:S(2)}) %copy-start) | copy-done | bytes 8388632
  76.9 3.4 %copy-done.2 = bf16[1024,4096]{1,0:T(8,128)(2,1)S(1)} copy-done((bf16[1024,4096]{1,0:T(8,128)(2,1)S(1)}, bf16[1024,4096]{1,0:T(8,128)(2,1)}, u32[]{:S(2)}) %copy-start.2) | copy-done | bytes 8388632
  80.3 8.0 %shard_map.479 = (bf16[48,4096]{1,0:T(8,128)(2,1)S(1)}, bf16[32,4096]{1,0:T(8,128)(2,1)S(1)}) custom-call(s32[8]{0:T(128)S(1)} %dynamic-slice_bitcast_fusion.refs_0_, bf16[48,4096]{1,0:T(8,128)(2,1)} %collective-permute-done.22.refs_1_, bf16[32,4096]{1,0:T(8,128)(2,1)} %collective-permute-done.23.refs_2_, bf16[4096,1024]{1,0:T(8,128)(2,1)S(1)} %copy-done, ...), custom_call_target="tpu_custom_call" | custom-call | flops 1509949440 | bytes 20971520 | tf_op jit(solution)/shard_map/pallas_call | solution.py:272
  88.3 0.8 collective-permute-start.24
  89.1 1.3 collective-permute-start.25
  90.4 8.0 %shard_map.474 = (bf16[32,4096]{1,0:T(8,128)(2,1)S(1)}, bf16[48,4096]{1,0:T(8,128)(2,1)S(1)}) custom-call(s32[8]{0:T(128)S(1)} %dynamic-slice_bitcast_fusion.refs_0_, bf16[32,4096]{1,0:T(8,128)(2,1)} %collective-permute-done.7.refs_1_, bf16[48,4096]{1,0:T(8,128)(2,1)} %collective-permute-done.8.refs_2_, bf16[4096,1024]{1,0:T(8,128)(2,1)S(1)} %copy-done, ...), custom_call_target="tpu_custom_call" | custom-call | flops 1509949440 | bytes 20971520 | tf_op jit(solution)/shard_map/pallas_call | solution.py:272
  98.5 2.2 %collective-permute-start.9 = (bf16[32,4096]{1,0:T(8,128)(2,1)S(1)}, bf16[32,4096]{1,0:T(8,128)(2,1)S(1)}, u32[]{:S(2)}, u32[]{:S(2)}) collective-permute-start(bf16[32,4096]{1,0:T(8,128)(2,1)S(1)} %get-tuple-element.37), channel_id=1, source_target_pairs={{0,3},{1,0},{2,1},{3,2},{4,7},{5,4},{6,5},{7,6},{8,11},{9,8},{10,9... | collective-permute-start | bytes 786440 | tf_op jit(solution)/shard_map/ppermute | solution.py:410
  100.7 14.7 %shard_map.478 = (bf16[80,4096]{1,0:T(8,128)(2,1)S(1)}, bf16[80,4096]{1,0:T(8,128)(2,1)S(1)}, bf16[80,4096]{1,0:T(8,128)(2,1)S(1)}) custom-call(s32[8]{0:T(128)S(1)} %dynamic-slice_bitcast_fusion.refs_0_, bf16[80,4096]{1,0:T(8,128)(2,1)S(1)} %copy-done.16, bf16[80,4096]{1,0:T(8,128)(2,1)S(1)} %copy-done.21, ...), custom_call_target="tpu_custom_call" | custom-call | flops 4529848320 | bytes 20971520 | tf_op jit(solution)/shard_map/pallas_call | solution.py:272
  115.5 3.2 %collective-permute-start.27 = (bf16[80,4096]{1,0:T(8,128)(2,1)S(1)}, bf16[80,4096]{1,0:T(8,128)(2,1)S(1)}, u32[]{:S(2)}, u32[]{:S(2)}) collective-permute-start(bf16[80,4096]{1,0:T(8,128)(2,1)S(1)} %get-tuple-element.52), channel_id=1, source_target_pairs={{0,3},{1,0},{2,1},{3,2},{4,7},{5,4},{6,5},{7,6},{8,11},{9,8},{10,9... | collective-permute-start | bytes 1966088 | tf_op jit(solution)/shard_map/ppermute | solution.py:410
  119.0 1.6 collective-permute-start.26
  120.6 13.3 %shard_map.473 = (bf16[80,4096]{1,0:T(8,128)(2,1)S(1)}, bf16[80,4096]{1,0:T(8,128)(2,1)S(1)}, bf16[80,4096]{1,0:T(8,128)(2,1)S(1)}) custom-call(s32[8]{0:T(128)S(1)} %dynamic-slice_bitcast_fusion.refs_0_, bf16[80,4096]{1,0:T(8,128)(2,1)S(1)} %copy-done.19, bf16[80,4096]{1,0:T(8,128)(2,1)S(1)} %copy-done.14, ...), custom_call_target="tpu_custom_call" | custom-call | flops 4529848320 | bytes 20971520 | tf_op jit(solution)/shard_map/pallas_call | solution.py:272
  133.9 4.9 %collective-permute-done.10.refs_3_ = bf16[48,4096]{1,0:T(8,128)(2,1)S(1)} collective-permute-done((bf16[48,4096]{1,0:T(8,128)(2,1)S(1)}, bf16[48,4096]{1,0:T(8,128)(2,1)S(1)}, u32[]{:S(2)}, u32[]{:S(2)}) %collective-permute-start.10) | collective-permute-done | bytes 393248 | tf_op jit(solution)/shard_map/ppermute | solution.py:410
  139.0 1.7 collective-permute-start.28
  140.7 1.5 collective-permute-start.11
  142.2 1.7 collective-permute-start.13
  143.9 14.8 %shard_map.477 = (bf16[80,4096]{1,0:T(8,128)(2,1)}, bf16[80,4096]{1,0:T(8,128)(2,1)S(1)}, bf16[80,4096]{1,0:T(8,128)(2,1)}) custom-call(s32[8]{0:T(128)S(1)} %dynamic-slice_bitcast_fusion.refs_0_, bf16[80,4096]{1,0:T(8,128)(2,1)} %collective-permute-done.16.refs_1_, bf16[80,4096]{1,0:T(8,128)(2,1)S(1)} %collective-permute-done.17.refs_2_, ...), custom_call_target="tpu_custom_call" | custom-call | flops 4529848320 | bytes 20971520 | tf_op jit(solution)/shard_map/pallas_call | solution.py:272
  158.8 0.4 collective-permute-start.30
  159.2 14.5 %shard_map.472 = (bf16[80,4096]{1,0:T(8,128)(2,1)}, bf16[80,4096]{1,0:T(8,128)(2,1)}, bf16[80,4096]{1,0:T(8,128)(2,1)}) custom-call(s32[8]{0:T(128)S(1)} %dynamic-slice_bitcast_fusion.refs_0_, bf16[80,4096]{1,0:T(8,128)(2,1)S(1)} %collective-permute-done.refs_1_, bf16[80,4096]{1,0:T(8,128)(2,1)S(1)} %copy-done.24, bf16[80,4096]{1,0:T(8,128)(2,1)S(1)} %copy-done.26, ...), custom_call_target="tpu_custom_call" | custom-call | flops 4529848320 | bytes 20971520 | tf_op jit(solution)/shard_map/pallas_call | solution.py:272
  173.7 3.0 %collective-permute-start.3 = (bf16[80,4096]{1,0:T(8,128)(2,1)}, bf16[80,4096]{1,0:T(8,128)(2,1)}, u32[]{:S(2)}, u32[]{:S(2)}) collective-permute-start(bf16[80,4096]{1,0:T(8,128)(2,1)} %get-tuple-element.32), channel_id=1, source_target_pairs={{0,3},{1,0},{2,1},{3,2},{4,7},{5,4},{6,5},{7,6},{8,11},{9,8},{10,9... | collective-permute-start | bytes 1966088 | tf_op jit(solution)/shard_map/ppermute | solution.py:410
  176.7 2.8 %shard_map.481 = (bf16[80,4096]{1,0:T(8,128)(2,1)}, bf16[80,4096]{1,0:T(8,128)(2,1)}) custom-call(bf16[80,4096]{1,0:T(8,128)(2,1)} %get-tuple-element.45.refs_0_, bf16[80,4096]{1,0:T(8,128)(2,1)} %get-tuple-element.46.refs_1_, bf16[80,4096]{1,0:T(8,128)(2,1)S(1)} %collective-permute-done.26.refs_2_, ...), custom_call_target="tpu_custom_call", output_to_operand_aliasing={{0}: (0, {}), {1}: (1, {})} | custom-call | flops 41943040 | bytes 1966080 | tf_op jit(solution)/shard_map/pallas_call | solution.py:307
  179.5 0.7 collective-permute-start.29
  180.2 0.7 collective-permute-start.31
  180.9 2.8 %shard_map.476 = (bf16[80,4096]{1,0:T(8,128)(2,1)}, bf16[80,4096]{1,0:T(8,128)(2,1)}) custom-call(bf16[80,4096]{1,0:T(8,128)(2,1)} %get-tuple-element.33.refs_0_, bf16[80,4096]{1,0:T(8,128)(2,1)} %get-tuple-element.34.refs_1_, bf16[80,4096]{1,0:T(8,128)(2,1)S(1)} %collective-permute-done.11.refs_2_, ...), custom_call_target="tpu_custom_call", output_to_operand_aliasing={{0}: (0, {}), {1}: (1, {})} | custom-call | flops 41943040 | bytes 1966080 | tf_op jit(solution)/shard_map/pallas_call | solution.py:307
  183.7 1.3 collective-permute-start.14
  185.0 0.9 copy-done.29
  185.9 1.4 collective-permute-start.15
  187.2 1.5 constant_dynamic-slice_fusion.refs_1_
  188.8 3.4 %copy-done.1 = bf16[4096,1024]{1,0:T(8,128)(2,1)S(1)} copy-done((bf16[4096,1024]{1,0:T(8,128)(2,1)S(1)}, bf16[4096,1024]{1,0:T(8,128)(2,1)}, u32[]{:S(2)}) %copy-start.1) | copy-done | bytes 8388632
  192.1 3.4 %copy-done.3 = bf16[1024,4096]{1,0:T(8,128)(2,1)S(1)} copy-done((bf16[1024,4096]{1,0:T(8,128)(2,1)S(1)}, bf16[1024,4096]{1,0:T(8,128)(2,1)}, u32[]{:S(2)}) %copy-start.3) | copy-done | bytes 8388632
  195.5 1.1 copy-done.10
  196.6 9.8 %shard_map.471 = (bf16[80,4096]{1,0:T(8,128)(2,1)S(1)}, bf16[80,4096]{1,0:T(8,128)(2,1)S(1)}) custom-call(s32[8]{0:T(128)S(1)} %dynamic-slice_bitcast_fusion.refs_0_, bf16[80,4096]{1,0:T(8,128)(2,1)S(1)} %shard_map.469.refs_1_, bf16[80,4096]{1,0:T(8,128)(2,1)S(1)} %copy-done.10, bf16[4096,1024]{1,0:T(8,128)(2,1)S(1)} %copy-done.1, ...), custom_call_target="tpu_custom_call" | custom-call | flops 3019898880 | bytes 20971520 | tf_op jit(solution)/shard_map/pallas_call | solution.py:272
  206.5 3.8 %shard_map.482.refs_6_ = bf16[160,4096]{1,0:T(8,128)(2,1)} custom-call(bf16[160,4096]{1,0:T(8,128)(2,1)} %refs_0_.7, s32[160,32]{1,0:T(8,128)} %constant_dynamic-slice_fusion.refs_1_, bf16[80,4096]{1,0:T(8,128)(2,1)S(1)} %get-tuple-element.44.refs_2_, bf16[80,4096]{1,0:T(8,128)(2,1)} %collective-permute-done.29.refs_3_, bf16[80,4096]{1,0:T(8,128)(2,1)S(1)} %copy-done.30, ...), custom_call_target="tpu_custom_call" | custom-call | flops 20971520 | bytes 3932160 | tf_op jit(solution)/shard_map/pallas_call | solution.py:370
  210.4 4.0 %shard_map.483 = bf16[160,4096]{1,0:T(8,128)(2,1)} custom-call(bf16[160,4096]{1,0:T(8,128)(2,1)} %refs_0_.7, s32[160,32]{1,0:T(8,128)} %constant_dynamic-slice_fusion.refs_1_, bf16[80,4096]{1,0:T(8,128)(2,1)S(1)} %get-tuple-element.31.refs_2_, bf16[80,4096]{1,0:T(8,128)(2,1)} %collective-permute-done.3.refs_3_, ...), custom_call_target="tpu_custom_call", output_to_operand_aliasing={{}: (6, {})} | custom-call | flops 20971520 | bytes 3932160 | tf_op jit(solution)/shard_map/pallas_call | solution.py:370
  (89 shorter events, 0.7 us)
Async XLA Ops:
  0.0 73.5 %copy-start.11 = (f32[80,128]{1,0:T(8,128)S(1)}, f32[80,128]{1,0:T(8,128)}, u32[]{:S(2)}) copy-start(f32[80,128]{1,0:T(8,128)} %constant.30.clone.refs_9_.refs_10_) | copy-start | bytes 122884
  0.0 73.5 %copy-start.12 = (f32[80,128]{1,0:T(8,128)S(1)}, f32[80,128]{1,0:T(8,128)}, u32[]{:S(2)}) copy-start(f32[80,128]{1,0:T(8,128)} %constant.31.clone.refs_10_.refs_11_) | copy-start | bytes 122884
  0.0 73.5 %copy-start.17 = (bf16[128,80]{1,0:T(8,128)(2,1)S(1)}, bf16[128,80]{1,0:T(8,128)(2,1)}, u32[]{:S(2)}) copy-start(bf16[128,80]{1,0:T(8,128)(2,1)} %constant.32.clone.refs_11_.refs_12_) | copy-start | bytes 61444
  0.0 73.5 %copy-start.22 = (bf16[80,128]{1,0:T(8,128)(2,1)S(1)}, bf16[80,128]{1,0:T(8,128)(2,1)}, u32[]{:S(2)}) copy-start(bf16[80,128]{1,0:T(8,128)(2,1)} %constant.33.clone.refs_12_.refs_13_) | copy-start | bytes 61444
  0.0 73.5 %copy-start.6 = (bf16[1024,80]{1,0:T(8,128)(2,1)S(1)}, bf16[1024,80]{1,0:T(8,128)(2,1)}, u32[]{:S(2)}) copy-start(bf16[1024,80]{1,0:T(8,128)(2,1)} %constant.34.clone.refs_13_.refs_14_) | copy-start | bytes 491524
  0.0 73.5 %copy-start.7 = (bf16[4,32,1024]{2,1,0:T(8,128)(2,1)S(1)}, bf16[4,32,1024]{2,1,0:T(8,128)(2,1)}, u32[]{:S(2)}) copy-start(bf16[4,32,1024]{2,1,0:T(8,128)(2,1)} %constant.35.clone.refs_14_.refs_15_) | copy-start | bytes 786436
  0.0 73.5 %copy-start.4 = (bf16[4096,128]{1,0:T(8,128)(2,1)S(1)}, bf16[4096,128]{1,0:T(8,128)(2,1)}, u32[]{:S(2)}) copy-start(bf16[4096,128]{1,0:T(8,128)(2,1)} %refs_4_.13) | copy-start | bytes 3145732
  0.0 73.5 %copy-start.5 = (bf16[4096,128]{1,0:T(8,128)(2,1)S(1)}, bf16[4096,128]{1,0:T(8,128)(2,1)}, u32[]{:S(2)}) copy-start(bf16[4096,128]{1,0:T(8,128)(2,1)} %refs_5_.13) | copy-start | bytes 3145732
  2.0 18.1 %collective-permute-start.16 = (bf16[80,4096]{1,0:T(8,128)(2,1)S(1)}, bf16[80,4096]{1,0:T(8,128)(2,1)}, u32[]{:S(2)}, u32[]{:S(2)}) collective-permute-start(bf16[80,4096]{1,0:T(8,128)(2,1)S(1)} %shard_map.469.refs_1_), channel_id=1, source_target_pairs={{0,1},{1,2},{2,3},{3,0},{4,5},{5,6},{6,7},{7,4},{8,9},{9,10},{10,1... | collective-permute-start | bytes 1966088 | tf_op jit(solution)/shard_map/ppermute | solution.py:410
  3.7 17.8 %collective-permute-start.18 = (bf16[80,4096]{1,0:T(8,128)(2,1)S(1)}, bf16[80,4096]{1,0:T(8,128)(2,1)S(1)}, u32[]{:S(2)}, u32[]{:S(2)}) collective-permute-start(bf16[80,4096]{1,0:T(8,128)(2,1)S(1)} %shard_map.469.refs_1_), channel_id=1, source_target_pairs={{0,4},{1,5},{2,6},{3,7},{4,0},{5,1},{6,2},{7,3},{8,12},{9,13},{10,... | collective-permute-start | bytes 1966088 | tf_op jit(solution)/shard_map/ppermute | solution.py:410
  7.0 14.5 %copy-start.8 = (bf16[80,4096]{1,0:T(8,128)(2,1)}, bf16[80,4096]{1,0:T(8,128)(2,1)S(1)}, u32[]{:S(2)}) copy-start(bf16[80,4096]{1,0:T(8,128)(2,1)S(1)} %shard_map.470.refs_2_) | copy-start | bytes 1966084
  7.0 17.1 %collective-permute-start.1 = (bf16[80,4096]{1,0:T(8,128)(2,1)S(1)}, bf16[80,4096]{1,0:T(8,128)(2,1)S(1)}, u32[]{:S(2)}, u32[]{:S(2)}) collective-permute-start(bf16[80,4096]{1,0:T(8,128)(2,1)S(1)} %shard_map.470.refs_2_), channel_id=1, source_target_pairs={{0,3},{1,0},{2,1},{3,2},{4,7},{5,4},{6,5},{7,6},{8,11},{9,8},{10,9... | collective-permute-start | bytes 1966088 | tf_op jit(solution)/shard_map/ppermute | solution.py:410
  8.7 26.6 %collective-permute-start.2 = (bf16[80,4096]{1,0:T(8,128)(2,1)S(1)}, bf16[80,4096]{1,0:T(8,128)(2,1)S(1)}, u32[]{:S(2)}, u32[]{:S(2)}) collective-permute-start(bf16[80,4096]{1,0:T(8,128)(2,1)S(1)} %shard_map.470.refs_2_), channel_id=1, source_target_pairs={{0,4},{1,5},{2,6},{3,7},{4,0},{5,1},{6,2},{7,3},{8,12},{9,13},{10,... | collective-permute-start | bytes 1966088 | tf_op jit(solution)/shard_map/ppermute | solution.py:410
  20.0 29.4 %collective-permute-start.19 = (bf16[80,4096]{1,0:T(8,128)(2,1)}, bf16[80,4096]{1,0:T(8,128)(2,1)S(1)}, u32[]{:S(2)}, u32[]{:S(2)}) collective-permute-start(bf16[80,4096]{1,0:T(8,128)(2,1)} %collective-permute-done.16.refs_1_), channel_id=1, source_target_pairs={{0,4},{1,5},{2,6},{3,7},{4,0},{5,1},{6,2},{7,3},{8,12},{9,13},{10,... | collective-permute-start | bytes 1966088 | tf_op jit(solution)/shard_map/ppermute | solution.py:410
  21.5 31.6 %collective-permute-start.20 = (bf16[80,4096]{1,0:T(8,128)(2,1)S(1)}, bf16[80,4096]{1,0:T(8,128)(2,1)S(1)}, u32[]{:S(2)}, u32[]{:S(2)}) collective-permute-start(bf16[80,4096]{1,0:T(8,128)(2,1)S(1)} %collective-permute-done.18.refs_3_), channel_id=1, source_target_pairs={{0,3},{1,0},{2,1},{3,2},{4,7},{5,4},{6,5},{7,6},{8,11},{9,8},{10,9... | collective-permute-start | bytes 1966088 | tf_op jit(solution)/shard_map/ppermute | solution.py:410
  24.1 43.2 %copy-start.23 = (bf16[80,4096]{1,0:T(8,128)(2,1)}, bf16[80,4096]{1,0:T(8,128)(2,1)S(1)}, u32[]{:S(2)}) copy-start(bf16[80,4096]{1,0:T(8,128)(2,1)S(1)} %collective-permute-done.1.refs_2_) | copy-start | bytes 1966084
  24.1 38.0 %collective-permute-start.5 = (bf16[80,4096]{1,0:T(8,128)(2,1)S(1)}, bf16[80,4096]{1,0:T(8,128)(2,1)S(1)}, u32[]{:S(2)}, u32[]{:S(2)}) collective-permute-start(bf16[80,4096]{1,0:T(8,128)(2,1)S(1)} %collective-permute-done.1.refs_2_), channel_id=1, source_target_pairs={{0,4},{1,5},{2,6},{3,7},{4,0},{5,1},{6,2},{7,3},{8,12},{9,13},{10,... | collective-permute-start | bytes 1966088 | tf_op jit(solution)/shard_map/ppermute | solution.py:410
  35.4 30.1 %collective-permute-start.4 = (bf16[80,4096]{1,0:T(8,128)(2,1)S(1)}, bf16[80,4096]{1,0:T(8,128)(2,1)S(1)}, u32[]{:S(2)}, u32[]{:S(2)}) collective-permute-start(bf16[80,4096]{1,0:T(8,128)(2,1)S(1)} %collective-permute-done.2.refs_3_), channel_id=1, source_target_pairs={{0,1},{1,2},{2,3},{3,0},{4,5},{5,6},{6,7},{7,4},{8,9},{9,10},{10,1... | collective-permute-start | bytes 1966088 | tf_op jit(solution)/shard_map/ppermute | solution.py:410
  37.0 0.8 copy-start.25
  49.4 13.4 %copy-start.15 = (bf16[80,4096]{1,0:T(8,128)(2,1)}, bf16[80,4096]{1,0:T(8,128)(2,1)S(1)}, u32[]{:S(2)}) copy-start(bf16[80,4096]{1,0:T(8,128)(2,1)S(1)} %collective-permute-done.19.refs_1_) | copy-start | bytes 1966084
  50.3 22.7 %collective-permute-start.22 = (bf16[48,4096]{1,0:T(8,128)(2,1)}, bf16[48,4096]{1,0:T(8,128)(2,1)}, u32[]{:S(2)}, u32[]{:S(2)}) collective-permute-start(bf16[48,4096]{1,0:T(8,128)(2,1)} %slice.18), channel_id=1, source_target_pairs={{0,1},{1,2},{2,3},{3,0},{4,5},{5,6},{6,7},{7,4},{8,9},{9,10},{10,1... | collective-permute-start | bytes 1179656 | tf_op jit(solution)/shard_map/ppermute | solution.py:410
  51.9 46.6 %collective-permute-start.21 = (bf16[80,4096]{1,0:T(8,128)(2,1)}, bf16[80,4096]{1,0:T(8,128)(2,1)}, u32[]{:S(2)}, u32[]{:S(2)}) collective-permute-start(bf16[80,4096]{1,0:T(8,128)(2,1)} %collective-permute-done.16.refs_1_), channel_id=1, source_target_pairs={{0,1},{1,2},{2,3},{3,0},{4,5},{5,6},{6,7},{7,4},{8,9},{9,10},{10,1... | collective-permute-start | bytes 1966088 | tf_op jit(solution)/shard_map/ppermute | solution.py:410
  53.2 13.1 %copy-start.20 = (bf16[80,4096]{1,0:T(8,128)(2,1)}, bf16[80,4096]{1,0:T(8,128)(2,1)S(1)}, u32[]{:S(2)}) copy-start(bf16[80,4096]{1,0:T(8,128)(2,1)S(1)} %collective-permute-done.20.refs_2_) | copy-start | bytes 1966084
  53.9 16.0 %collective-permute-start.23 = (bf16[32,4096]{1,0:T(8,128)(2,1)}, bf16[32,4096]{1,0:T(8,128)(2,1)}, u32[]{:S(2)}, u32[]{:S(2)}) collective-permute-start(bf16[32,4096]{1,0:T(8,128)(2,1)} %slice.19), channel_id=1, source_target_pairs={{0,3},{1,0},{2,1},{3,2},{4,7},{5,4},{6,5},{7,6},{8,11},{9,8},{10,9... | collective-permute-start | bytes 786440 | tf_op jit(solution)/shard_map/ppermute | solution.py:410
  62.9 0.8 copy-start.13
  63.7 25.4 %collective-permute-start.8 = (bf16[48,4096]{1,0:T(8,128)(2,1)}, bf16[48,4096]{1,0:T(8,128)(2,1)}, u32[]{:S(2)}, u32[]{:S(2)}) collective-permute-start(bf16[48,4096]{1,0:T(8,128)(2,1)} %slice.17), channel_id=1, source_target_pairs={{0,3},{1,0},{2,1},{3,2},{4,7},{5,4},{6,5},{7,6},{8,11},{9,8},{10,9... | collective-permute-start | bytes 1179656 | tf_op jit(solution)/shard_map/ppermute | solution.py:410
  66.2 0.8 copy-start.18
  67.1 21.2 %collective-permute-start.7 = (bf16[32,4096]{1,0:T(8,128)(2,1)}, bf16[32,4096]{1,0:T(8,128)(2,1)}, u32[]{:S(2)}, u32[]{:S(2)}) collective-permute-start(bf16[32,4096]{1,0:T(8,128)(2,1)} %slice.16), channel_id=1, source_target_pairs={{0,1},{1,2},{2,3},{3,0},{4,5},{5,6},{6,7},{7,4},{8,9},{9,10},{10,1... | collective-permute-start | bytes 786440 | tf_op jit(solution)/shard_map/ppermute | solution.py:410
  70.0 69.0 %collective-permute-start.17 = (bf16[80,4096]{1,0:T(8,128)(2,1)S(1)}, bf16[80,4096]{1,0:T(8,128)(2,1)S(1)}, u32[]{:S(2)}, u32[]{:S(2)}) collective-permute-start(bf16[80,4096]{1,0:T(8,128)(2,1)S(1)} %shard_map.469.refs_1_), channel_id=1, source_target_pairs={{0,3},{1,0},{2,1},{3,2},{4,7},{5,4},{6,5},{7,6},{8,11},{9,8},{10,9... | collective-permute-start | bytes 1966088 | tf_op jit(solution)/shard_map/ppermute | solution.py:410
  73.0 45.9 %collective-permute-start.6 = (bf16[80,4096]{1,0:T(8,128)(2,1)}, bf16[80,4096]{1,0:T(8,128)(2,1)S(1)}, u32[]{:S(2)}, u32[]{:S(2)}) collective-permute-start(bf16[80,4096]{1,0:T(8,128)(2,1)} %copy-done.23), channel_id=1, source_target_pairs={{0,3},{1,0},{2,1},{3,2},{4,7},{5,4},{6,5},{7,6},{8,11},{9,8},{10,9... | collective-permute-start | bytes 1966088 | tf_op jit(solution)/shard_map/ppermute | solution.py:410
  73.5 3.4 %copy-start = (bf16[4096,1024]{1,0:T(8,128)(2,1)S(1)}, bf16[4096,1024]{1,0:T(8,128)(2,1)}, u32[]{:S(2)}) copy-start(bf16[4096,1024]{1,0:T(8,128)(2,1)} %refs_3_.5) | copy-start | bytes 25165828
  76.9 3.4 %copy-start.2 = (bf16[1024,4096]{1,0:T(8,128)(2,1)S(1)}, bf16[1024,4096]{1,0:T(8,128)(2,1)}, u32[]{:S(2)}) copy-start(bf16[1024,4096]{1,0:T(8,128)(2,1)} %refs_6_.13) | copy-start | bytes 25165828
  88.3 27.2 %collective-permute-start.24 = (bf16[48,4096]{1,0:T(8,128)(2,1)S(1)}, bf16[48,4096]{1,0:T(8,128)(2,1)S(1)}, u32[]{:S(2)}, u32[]{:S(2)}) collective-permute-start(bf16[48,4096]{1,0:T(8,128)(2,1)S(1)} %get-tuple-element.49), channel_id=1, source_target_pairs={{0,3},{1,0},{2,1},{3,2},{4,7},{5,4},{6,5},{7,6},{8,11},{9,8},{10,9... | collective-permute-start | bytes 1179656 | tf_op jit(solution)/shard_map/ppermute | solution.py:410
  89.1 11.6 %copy-start.16 = (bf16[80,4096]{1,0:T(8,128)(2,1)S(1)}, bf16[80,4096]{1,0:T(8,128)(2,1)}, u32[]{:S(2)}) copy-start(bf16[80,4096]{1,0:T(8,128)(2,1)} %copy-done.15) | copy-start | bytes 1966084
  89.1 11.6 %copy-start.21 = (bf16[80,4096]{1,0:T(8,128)(2,1)S(1)}, bf16[80,4096]{1,0:T(8,128)(2,1)}, u32[]{:S(2)}) copy-start(bf16[80,4096]{1,0:T(8,128)(2,1)} %copy-done.20) | copy-start | bytes 1966084
  89.1 26.3 %collective-permute-start.25 = (bf16[32,4096]{1,0:T(8,128)(2,1)S(1)}, bf16[32,4096]{1,0:T(8,128)(2,1)S(1)}, u32[]{:S(2)}, u32[]{:S(2)}) collective-permute-start(bf16[32,4096]{1,0:T(8,128)(2,1)S(1)} %get-tuple-element.50), channel_id=1, source_target_pairs={{0,1},{1,2},{2,3},{3,0},{4,5},{5,6},{6,7},{7,4},{8,9},{9,10},{10,1... | collective-permute-start | bytes 786440 | tf_op jit(solution)/shard_map/ppermute | solution.py:410
  98.5 22.1 %slice-start = ((s8[8388608]{0:T(1024)(128)(4,1)}), s8[4194304]{0:T(1024)(128)(4,1)S(1)}, s32[]{:S(2)}) async-start(s8[8388608]{0:T(1024)(128)(4,1)} %bitcast.4), calls=%async_computation | async-start | bytes 8388608
  98.5 16.9 %copy-start.9 = (bf16[80,4096]{1,0:T(8,128)(2,1)S(1)}, bf16[80,4096]{1,0:T(8,128)(2,1)}, u32[]{:S(2)}) copy-start(bf16[80,4096]{1,0:T(8,128)(2,1)} %copy-done.8) | copy-start | bytes 1966084
  98.5 22.1 %slice-start.1 = ((s8[8388608]{0:T(1024)(128)(4,1)}), s8[4194304]{0:T(1024)(128)(4,1)S(1)}, s32[]{:S(2)}) async-start(s8[8388608]{0:T(1024)(128)(4,1)} %bitcast.4), calls=%async_computation.1 | async-start | bytes 8388608
  98.5 22.1 %copy-start.14 = (bf16[80,4096]{1,0:T(8,128)(2,1)S(1)}, bf16[80,4096]{1,0:T(8,128)(2,1)}, u32[]{:S(2)}) copy-start(bf16[80,4096]{1,0:T(8,128)(2,1)} %copy-done.13) | copy-start | bytes 1966084
  98.5 22.1 %copy-start.19 = (bf16[80,4096]{1,0:T(8,128)(2,1)S(1)}, bf16[80,4096]{1,0:T(8,128)(2,1)}, u32[]{:S(2)}) copy-start(bf16[80,4096]{1,0:T(8,128)(2,1)} %copy-done.18) | copy-start | bytes 1966084
  98.5 20.5 %collective-permute-start.9 = (bf16[32,4096]{1,0:T(8,128)(2,1)S(1)}, bf16[32,4096]{1,0:T(8,128)(2,1)S(1)}, u32[]{:S(2)}, u32[]{:S(2)}) collective-permute-start(bf16[32,4096]{1,0:T(8,128)(2,1)S(1)} %get-tuple-element.37), channel_id=1, source_target_pairs={{0,3},{1,0},{2,1},{3,2},{4,7},{5,4},{6,5},{7,6},{8,11},{9,8},{10,9... | collective-permute-start | bytes 786440 | tf_op jit(solution)/shard_map/ppermute | solution.py:410
  115.4 25.3 %collective-permute-start = (bf16[80,4096]{1,0:T(8,128)(2,1)S(1)}, bf16[80,4096]{1,0:T(8,128)(2,1)S(1)}, u32[]{:S(2)}, u32[]{:S(2)}) collective-permute-start(bf16[80,4096]{1,0:T(8,128)(2,1)S(1)} %copy-done.9), channel_id=1, source_target_pairs={{0,1},{1,2},{2,3},{3,0},{4,5},{5,6},{6,7},{7,4},{8,9},{9,10},{10,1... | collective-permute-start | bytes 1966088 | tf_op jit(solution)/shard_map/ppermute | solution.py:410
  115.5 26.7 %collective-permute-start.27 = (bf16[80,4096]{1,0:T(8,128)(2,1)S(1)}, bf16[80,4096]{1,0:T(8,128)(2,1)S(1)}, u32[]{:S(2)}, u32[]{:S(2)}) collective-permute-start(bf16[80,4096]{1,0:T(8,128)(2,1)S(1)} %get-tuple-element.52), channel_id=1, source_target_pairs={{0,3},{1,0},{2,1},{3,2},{4,7},{5,4},{6,5},{7,6},{8,11},{9,8},{10,9... | collective-permute-start | bytes 1966088 | tf_op jit(solution)/shard_map/ppermute | solution.py:410
  118.9 19.9 %collective-permute-start.10 = (bf16[48,4096]{1,0:T(8,128)(2,1)S(1)}, bf16[48,4096]{1,0:T(8,128)(2,1)S(1)}, u32[]{:S(2)}, u32[]{:S(2)}) collective-permute-start(bf16[48,4096]{1,0:T(8,128)(2,1)S(1)} %get-tuple-element.38), channel_id=1, source_target_pairs={{0,1},{1,2},{2,3},{3,0},{4,5},{5,6},{6,7},{7,4},{8,9},{9,10},{10,1... | collective-permute-start | bytes 1179656 | tf_op jit(solution)/shard_map/ppermute | solution.py:410
  119.0 24.9 %copy-start.28 = (bf16[80,4096]{1,0:T(8,128)(2,1)S(1)}, bf16[80,4096]{1,0:T(8,128)(2,1)}, u32[]{:S(2)}) copy-start(bf16[80,4096]{1,0:T(8,128)(2,1)} %copy-done.27) | copy-start | bytes 1966084
  119.0 39.8 %collective-permute-start.26 = (bf16[80,4096]{1,0:T(8,128)(2,1)S(1)}, bf16[80,4096]{1,0:T(8,128)(2,1)S(1)}, u32[]{:S(2)}, u32[]{:S(2)}) collective-permute-start(bf16[80,4096]{1,0:T(8,128)(2,1)S(1)} %get-tuple-element.51), channel_id=1, source_target_pairs={{0,4},{1,5},{2,6},{3,7},{4,0},{5,1},{6,2},{7,3},{8,12},{9,13},{10,... | collective-permute-start | bytes 1966088 | tf_op jit(solution)/shard_map/ppermute | solution.py:410
  138.8 40.7 %collective-permute-start.12 = (bf16[80,4096]{1,0:T(8,128)(2,1)S(1)}, bf16[80,4096]{1,0:T(8,128)(2,1)S(1)}, u32[]{:S(2)}, u32[]{:S(2)}) collective-permute-start(bf16[80,4096]{1,0:T(8,128)(2,1)S(1)} %get-tuple-element.40), channel_id=1, source_target_pairs={{0,1},{1,2},{2,3},{3,0},{4,5},{5,6},{6,7},{7,4},{8,9},{9,10},{10,1... | collective-permute-start | bytes 1966088 | tf_op jit(solution)/shard_map/ppermute | solution.py:410
  139.0 34.7 %collective-permute-start.28 = (bf16[80,4096]{1,0:T(8,128)(2,1)S(1)}, bf16[80,4096]{1,0:T(8,128)(2,1)S(1)}, u32[]{:S(2)}, u32[]{:S(2)}) collective-permute-start(bf16[80,4096]{1,0:T(8,128)(2,1)S(1)} %get-tuple-element.53), channel_id=1, source_target_pairs={{0,1},{1,2},{2,3},{3,0},{4,5},{5,6},{6,7},{7,4},{8,9},{9,10},{10,1... | collective-permute-start | bytes 1966088 | tf_op jit(solution)/shard_map/ppermute | solution.py:410
  140.7 39.5 %collective-permute-start.11 = (bf16[80,4096]{1,0:T(8,128)(2,1)S(1)}, bf16[80,4096]{1,0:T(8,128)(2,1)S(1)}, u32[]{:S(2)}, u32[]{:S(2)}) collective-permute-start(bf16[80,4096]{1,0:T(8,128)(2,1)S(1)} %get-tuple-element.39), channel_id=1, source_target_pairs={{0,4},{1,5},{2,6},{3,7},{4,0},{5,1},{6,2},{7,3},{8,12},{9,13},{10,... | collective-permute-start | bytes 1966088 | tf_op jit(solution)/shard_map/ppermute | solution.py:410
  142.2 17.0 %copy-start.24 = (bf16[80,4096]{1,0:T(8,128)(2,1)S(1)}, bf16[80,4096]{1,0:T(8,128)(2,1)}, u32[]{:S(2)}) copy-start(bf16[80,4096]{1,0:T(8,128)(2,1)} %copy-done.23) | copy-start | bytes 1966084
  142.2 17.0 %copy-start.26 = (bf16[80,4096]{1,0:T(8,128)(2,1)S(1)}, bf16[80,4096]{1,0:T(8,128)(2,1)}, u32[]{:S(2)}) copy-start(bf16[80,4096]{1,0:T(8,128)(2,1)} %copy-done.25) | copy-start | bytes 1966084
  142.2 38.6 %collective-permute-start.13 = (bf16[80,4096]{1,0:T(8,128)(2,1)S(1)}, bf16[80,4096]{1,0:T(8,128)(2,1)S(1)}, u32[]{:S(2)}, u32[]{:S(2)}) collective-permute-start(bf16[80,4096]{1,0:T(8,128)(2,1)S(1)} %get-tuple-element.41), channel_id=1, source_target_pairs={{0,3},{1,0},{2,1},{3,2},{4,7},{5,4},{6,5},{7,6},{8,11},{9,8},{10,9... | collective-permute-start | bytes 1966088 | tf_op jit(solution)/shard_map/ppermute | solution.py:410
  158.8 26.2 %collective-permute-start.30 = (bf16[80,4096]{1,0:T(8,128)(2,1)S(1)}, bf16[80,4096]{1,0:T(8,128)(2,1)S(1)}, u32[]{:S(2)}, u32[]{:S(2)}) collective-permute-start(bf16[80,4096]{1,0:T(8,128)(2,1)S(1)} %get-tuple-element.55), channel_id=1, source_target_pairs={{0,1},{1,2},{2,3},{3,0},{4,5},{5,6},{6,7},{7,4},{8,9},{9,10},{10,1... | collective-permute-start | bytes 1966088 | tf_op jit(solution)/shard_map/ppermute | solution.py:410
  173.7 36.6 %collective-permute-start.3 = (bf16[80,4096]{1,0:T(8,128)(2,1)}, bf16[80,4096]{1,0:T(8,128)(2,1)}, u32[]{:S(2)}, u32[]{:S(2)}) collective-permute-start(bf16[80,4096]{1,0:T(8,128)(2,1)} %get-tuple-element.32), channel_id=1, source_target_pairs={{0,3},{1,0},{2,1},{3,2},{4,7},{5,4},{6,5},{7,6},{8,11},{9,8},{10,9... | collective-permute-start | bytes 1966088 | tf_op jit(solution)/shard_map/ppermute | solution.py:410
  179.5 26.9 %collective-permute-start.29 = (bf16[80,4096]{1,0:T(8,128)(2,1)}, bf16[80,4096]{1,0:T(8,128)(2,1)}, u32[]{:S(2)}, u32[]{:S(2)}) collective-permute-start(bf16[80,4096]{1,0:T(8,128)(2,1)} %get-tuple-element.54), channel_id=1, source_target_pairs={{0,3},{1,0},{2,1},{3,2},{4,7},{5,4},{6,5},{7,6},{8,11},{9,8},{10,9... | collective-permute-start | bytes 1966088 | tf_op jit(solution)/shard_map/ppermute | solution.py:410
  180.2 26.2 %collective-permute-start.31 = (bf16[80,4096]{1,0:T(8,128)(2,1)}, bf16[80,4096]{1,0:T(8,128)(2,1)}, u32[]{:S(2)}, u32[]{:S(2)}) collective-permute-start(bf16[80,4096]{1,0:T(8,128)(2,1)} %get-tuple-element.56), channel_id=1, source_target_pairs={{0,4},{1,5},{2,6},{3,7},{4,0},{5,1},{6,2},{7,3},{8,12},{9,13},{10,... | collective-permute-start | bytes 1966088 | tf_op jit(solution)/shard_map/ppermute | solution.py:410
  183.7 26.7 %collective-permute-start.14 = (bf16[80,4096]{1,0:T(8,128)(2,1)}, bf16[80,4096]{1,0:T(8,128)(2,1)}, u32[]{:S(2)}, u32[]{:S(2)}) collective-permute-start(bf16[80,4096]{1,0:T(8,128)(2,1)} %get-tuple-element.42), channel_id=1, source_target_pairs={{0,1},{1,2},{2,3},{3,0},{4,5},{5,6},{6,7},{7,4},{8,9},{9,10},{10,1... | collective-permute-start | bytes 1966088 | tf_op jit(solution)/shard_map/ppermute | solution.py:410
  185.0 0.9 copy-start.29
  185.9 24.5 %collective-permute-start.15 = (bf16[80,4096]{1,0:T(8,128)(2,1)}, bf16[80,4096]{1,0:T(8,128)(2,1)}, u32[]{:S(2)}, u32[]{:S(2)}) collective-permute-start(bf16[80,4096]{1,0:T(8,128)(2,1)} %get-tuple-element.43), channel_id=1, source_target_pairs={{0,4},{1,5},{2,6},{3,7},{4,0},{5,1},{6,2},{7,3},{8,12},{9,13},{10,... | collective-permute-start | bytes 1966088 | tf_op jit(solution)/shard_map/ppermute | solution.py:410
  188.8 3.4 %copy-start.1 = (bf16[4096,1024]{1,0:T(8,128)(2,1)S(1)}, bf16[4096,1024]{1,0:T(8,128)(2,1)}, u32[]{:S(2)}) copy-start(bf16[4096,1024]{1,0:T(8,128)(2,1)} %refs_3_.5) | copy-start | bytes 25165828
  192.1 3.4 %copy-start.3 = (bf16[1024,4096]{1,0:T(8,128)(2,1)S(1)}, bf16[1024,4096]{1,0:T(8,128)(2,1)}, u32[]{:S(2)}) copy-start(bf16[1024,4096]{1,0:T(8,128)(2,1)} %refs_6_.13) | copy-start | bytes 25165828
  195.5 1.1 copy-start.10
  196.6 9.9 %copy-start.30 = (bf16[80,4096]{1,0:T(8,128)(2,1)S(1)}, bf16[80,4096]{1,0:T(8,128)(2,1)}, u32[]{:S(2)}) copy-start(bf16[80,4096]{1,0:T(8,128)(2,1)} %copy-done.29) | copy-start | bytes 1966084
  (1 other events, 0.8 us)

commit v2 on v1

--- a/solution.py
+++ b/solution.py
@@ -282,6 +282,25 @@
     )
 
 
+def warm_kernel(offsets, *refs):
+    out = refs[-1]
+    for i in range(out.shape[0]):
+        out[i] = offsets[i]
+
+
+def warm(offsets, weights):
+    smem = pl.BlockSpec(memory_space=pltpu.SMEM)
+    inside = pl.BlockSpec(memory_space=VMEM)
+    return pl.pallas_call(
+        warm_kernel,
+        in_specs=[smem] + [inside] * len(weights),
+        out_specs=smem,
+        out_shape=jax.ShapeDtypeStruct(offsets.shape, offsets.dtype),
+        compiler_params=pltpu.CompilerParams(vmem_limit_bytes=LIMIT),
+        name="warm",
+    )(offsets, *weights)
+
+
 def add_kernel(jobs, *refs):
     count = len(jobs)
     bases, parts, outs = refs[:count], list(refs[count:-count]), refs[-count:]
@@ -317,13 +336,15 @@
     )(*[vmem(x) for x in (*bases, *parts)])
 
 
-def final_kernel(half, tokens, exps, *refs):
+def final_kernel(half, offsets, tokens, exps, *refs):
     (*parts, out, x, exponent, e, y, sems, out_sems) = refs
     parts = parts[:4]
     rows, width = parts[0].shape
     chunks = rows // CHUNK
     first = half * rows
-    e_copy = pltpu.make_async_copy(exps.at[pl.ds(first, rows)], exponent, sems.at[chunks])
+    e_copy = pltpu.make_async_copy(
+        exps.at[pl.ds(pl.multiple_of(offsets[OWN] + first, 8), rows)], exponent, sems.at[chunks]
+    )
     e_copy.start()
     for i in range(chunks):
         pltpu.make_async_copy(
@@ -357,11 +378,11 @@
         out_copy(i).wait()
 
 
-def final_half(tokens, exps, parts, half, previous=None):
+def final_half(offsets, tokens, exps, parts, half, previous=None):
     rows, width = parts[0].shape
     anywhere = pl.BlockSpec(memory_space=pl.ANY)
-    inputs = [hbm(tokens), hbm(exps), *[vmem(part) for part in parts]]
-    specs = [anywhere] * 2 + [pl.BlockSpec(memory_space=VMEM)] * len(parts)
+    inputs = [offsets, hbm(tokens), hbm(exps), *[vmem(part) for part in parts]]
+    specs = [pl.BlockSpec(memory_space=pltpu.SMEM)] + [anywhere] * 2 + [pl.BlockSpec(memory_space=VMEM)] * len(parts)
     aliases = {}
     if previous is not None:
         inputs.append(previous)
@@ -424,8 +445,8 @@
             vmem(weight) for weight in (query_weight, key_weight, value_weight, out_weight)
         ]
         weights = (*resident, hbm(cache), hbm(exponents))
+        offsets = warm(offsets, resident)
         gain = norm_gain.reshape(-1, HD)
-        own_exponents = lax.dynamic_slice_in_dim(exponents, index * own_rows, own_rows, 0)
 
         n0 = norm_half(tokens, gain, 0)
         a0, b0, c0 = move(n0, up), move(n0, down), move(n0, across)
@@ -459,8 +480,8 @@
         ga0, gb0, gc0 = move(pa0, down), move(pb0, up), move(pc0, across)
         pb1, pc1 = add_rows((pb1, 0, [fv1, fw1]), (pc1, 0, [fu1]))
         ga1, gb1, gc1 = move(pa1, down), move(pb1, up), move(pc1, across)
-        out = final_half(tokens, own_exponents, [own0, ga0, gb0, gc0], 0)
-        return final_half(tokens, own_exponents, [own1, ga1, gb1, gc1], 1, out)
+        out = final_half(offsets, tokens, exponents, [own0, ga0, gb0, gc0], 0)
+        return final_half(offsets, tokens, exponents, [own1, ga1, gb1, gc1], 1, out)
 
     return jax.shard_map(
         on_device,

time: 215 us -> 210 us (0.977)
  the two profiles are of different devices: /device:TPU:0 before, /device:TPU:24 now
where the time goes in v2:
time: 210 us
  Pallas kernels  92.2 us (44%)
  waiting for transfers between devices  53 us (25%)
  starting transfers between devices  44.2 us (21%)
  local copies, waits for them, and re-layouts  19.6 us (9%)
    pallas_call x7, Pallas kernels, block(): call(offsets, *[vmem(piece) for piece in pieces], *weights, jnp.asarray(c...  79.9 us
    ppermute x32, waiting for transfers between devices, move(): return lax.ppermute(value, 'tensor', where)  53 us
    ppermute x32, starting transfers between devices, move(): return lax.ppermute(value, 'tensor', where)  44.2 us
    unnamed x53, local copies, waits for them, and re-layouts  15.8 us
    pallas_call x2, Pallas kernels, final_half(): pl.pallas_call(lambda *refs: final_kernel(half, *refs), in_specs=specs, o...  6.23 us
  transfers between devices with their start and end apart: 32, of which 9 were waited for; matrix products, arithmetic and copies ran while one was open for 3% of the time, Pallas kernels for 42%

profile of v2, /device:TPU:24, one launch (start us, length us, event | category | flops | bytes accessed | tf_op | source)
XLA Modules:
  0.0 209.5 jit_solution(5701649351873028350)
XLA Ops:
  0.0 1.9 shard_map.469.refs_1_
  2.1 1.6 collective-permute-start.18
  3.7 1.8 shard_map.470.refs_2_
  5.5 1.9 collective-permute-start.1
  7.3 0.5 collective-permute-start.2
  7.9 10.7 %collective-permute-done.16.refs_1_ = bf16[80,4096]{1,0:T(8,128)(2,1)} collective-permute-done((bf16[80,4096]{1,0:T(8,128)(2,1)S(1)}, bf16[80,4096]{1,0:T(8,128)(2,1)}, u32[]{:S(2)}, u32[]{:S(2)}) %collective-permute-start.16) | collective-permute-done | bytes 655392 | tf_op jit(solution)/shard_map/ppermute | solution.py:431
  18.6 1.5 collective-permute-start.19
  20.1 1.6 collective-permute-start.20
  21.6 0.8 copy-done.24
  22.5 0.6 collective-permute-done.1.refs_2_
  23.0 0.9 collective-permute-start.5
  24.0 9.8 %collective-permute-done.2.refs_3_ = bf16[80,4096]{1,0:T(8,128)(2,1)S(1)} collective-permute-done((bf16[80,4096]{1,0:T(8,128)(2,1)S(1)}, bf16[80,4096]{1,0:T(8,128)(2,1)S(1)}, u32[]{:S(2)}, u32[]{:S(2)}) %collective-permute-start.2) | collective-permute-done | bytes 655392 | tf_op jit(solution)/shard_map/ppermute | solution.py:431
  33.7 1.7 collective-permute-start.4
  35.4 0.9 copy-done.22
  36.3 11.5 %collective-permute-done.19.refs_1_ = bf16[80,4096]{1,0:T(8,128)(2,1)S(1)} collective-permute-done((bf16[80,4096]{1,0:T(8,128)(2,1)}, bf16[80,4096]{1,0:T(8,128)(2,1)S(1)}, u32[]{:S(2)}, u32[]{:S(2)}) %collective-permute-start.19) | collective-permute-done | bytes 655392 | tf_op jit(solution)/shard_map/ppermute | solution.py:431
  47.8 0.8 slice.18
  48.6 1.7 collective-permute-start.22
  50.3 1.6 collective-permute-start.21
  51.9 0.8 slice.19
  52.7 0.4 collective-permute-start.23
  53.1 7.6 %collective-permute-done.5.refs_2_ = bf16[80,4096]{1,0:T(8,128)(2,1)S(1)} collective-permute-done((bf16[80,4096]{1,0:T(8,128)(2,1)S(1)}, bf16[80,4096]{1,0:T(8,128)(2,1)S(1)}, u32[]{:S(2)}, u32[]{:S(2)}) %collective-permute-start.5) | collective-permute-done | bytes 655392 | tf_op jit(solution)/shard_map/ppermute | solution.py:431
  60.7 0.8 slice.17
  61.5 0.9 copy-done.10
  62.3 1.7 collective-permute-start.8
  64.0 0.7 slice.16
  64.7 0.8 copy-done.15
  65.6 1.6 collective-permute-start.7
  67.2 2.0 copy.69.refs_8_.refs_9_.refs_2_
  69.2 0.7 dynamic-slice_bitcast_fusion.offsets
  69.9 3.4 %copy-done = bf16[4096,1024]{1,0:T(8,128)(2,1)S(1)} copy-done((bf16[4096,1024]{1,0:T(8,128)(2,1)S(1)}, bf16[4096,1024]{1,0:T(8,128)(2,1)}, u32[]{:S(2)}) %copy-start) | copy-done | bytes 8388632
  73.2 3.4 %copy-done.2 = bf16[1024,4096]{1,0:T(8,128)(2,1)S(1)} copy-done((bf16[1024,4096]{1,0:T(8,128)(2,1)S(1)}, bf16[1024,4096]{1,0:T(8,128)(2,1)}, u32[]{:S(2)}) %copy-start.2) | copy-done | bytes 8388632
  76.7 1.1 warm.1.refs_0_
  77.9 0.5 collective-permute-start.17
  78.4 0.7 collective-permute-start.6
  79.1 1.1 copy-done.1
  80.2 2.4 %copy-done.3 = bf16[1024,4096]{1,0:T(8,128)(2,1)S(1)} copy-done((bf16[1024,4096]{1,0:T(8,128)(2,1)S(1)}, bf16[1024,4096]{1,0:T(8,128)(2,1)}, u32[]{:S(2)}) %copy-start.3) | copy-done | bytes 8388632
  82.6 8.0 %shard_map.479 = (bf16[48,4096]{1,0:T(8,128)(2,1)S(1)}, bf16[32,4096]{1,0:T(8,128)(2,1)S(1)}) custom-call(s32[8]{0:T(128)S(1)} %warm.1.refs_0_, bf16[48,4096]{1,0:T(8,128)(2,1)} %collective-permute-done.22.refs_1_, bf16[32,4096]{1,0:T(8,128)(2,1)} %collective-permute-done.23.refs_2_, bf16[4096,1024]{1,0:T(8,128)(2,1)S(1)} %copy-done.1, ...), custom_call_target="tpu_custom_call" | custom-call | flops 1509949440 | bytes 20971520 | tf_op jit(solution)/shard_map/pallas_call | solution.py:272
  90.7 0.5 collective-permute-start.24
  91.2 2.8 %collective-permute-start.25 = (bf16[32,4096]{1,0:T(8,128)(2,1)S(1)}, bf16[32,4096]{1,0:T(8,128)(2,1)S(1)}, u32[]{:S(2)}, u32[]{:S(2)}) collective-permute-start(bf16[32,4096]{1,0:T(8,128)(2,1)S(1)} %get-tuple-element.50), channel_id=1, source_target_pairs={{0,1},{1,2},{2,3},{3,0},{4,5},{5,6},{6,7},{7,4},{8,9},{9,10},{10,1... | collective-permute-start | bytes 786440 | tf_op jit(solution)/shard_map/ppermute | solution.py:431
  94.0 8.0 %shard_map.474 = (bf16[32,4096]{1,0:T(8,128)(2,1)S(1)}, bf16[48,4096]{1,0:T(8,128)(2,1)S(1)}) custom-call(s32[8]{0:T(128)S(1)} %warm.1.refs_0_, bf16[32,4096]{1,0:T(8,128)(2,1)} %collective-permute-done.7.refs_1_, bf16[48,4096]{1,0:T(8,128)(2,1)} %collective-permute-done.8.refs_2_, bf16[4096,1024]{1,0:T(8,128)(2,1)S(1)} %copy-done.1, ...), custom_call_target="tpu_custom_call" | custom-call | flops 1509949440 | bytes 20971520 | tf_op jit(solution)/shard_map/pallas_call | solution.py:272
  102.3 13.9 %shard_map.478 = (bf16[80,4096]{1,0:T(8,128)(2,1)S(1)}, bf16[80,4096]{1,0:T(8,128)(2,1)S(1)}, bf16[80,4096]{1,0:T(8,128)(2,1)S(1)}) custom-call(s32[8]{0:T(128)S(1)} %warm.1.refs_0_, bf16[80,4096]{1,0:T(8,128)(2,1)S(1)} %copy-done.13, bf16[80,4096]{1,0:T(8,128)(2,1)S(1)} %copy-done.18, bf16[80,4096]{1,0:T(8,128)(2,1)} %collective-permute-done.21.refs_3_, ...), custom_call_target="tpu_custom_call" | custom-call | flops 4529848320 | bytes 20971520 | tf_op jit(solution)/shard_map/pallas_call | solution.py:272
  116.2 3.2 %collective-permute-start = (bf16[80,4096]{1,0:T(8,128)(2,1)S(1)}, bf16[80,4096]{1,0:T(8,128)(2,1)S(1)}, u32[]{:S(2)}, u32[]{:S(2)}) collective-permute-start(bf16[80,4096]{1,0:T(8,128)(2,1)S(1)} %shard_map.470.refs_2_), channel_id=1, source_target_pairs={{0,1},{1,2},{2,3},{3,0},{4,5},{5,6},{6,7},{7,4},{8,9},{9,10},{10,1... | collective-permute-start | bytes 1966088 | tf_op jit(solution)/shard_map/ppermute | solution.py:431
  119.6 3.3 %collective-permute-start.10 = (bf16[48,4096]{1,0:T(8,128)(2,1)S(1)}, bf16[48,4096]{1,0:T(8,128)(2,1)S(1)}, u32[]{:S(2)}, u32[]{:S(2)}) collective-permute-start(bf16[48,4096]{1,0:T(8,128)(2,1)S(1)} %get-tuple-element.38), channel_id=1, source_target_pairs={{0,1},{1,2},{2,3},{3,0},{4,5},{5,6},{6,7},{7,4},{8,9},{9,10},{10,1... | collective-permute-start | bytes 1179656 | tf_op jit(solution)/shard_map/ppermute | solution.py:431
  122.9 1.2 collective-permute-done.9.refs_2_
  124.1 1.4 collective-permute-start.26
  125.5 13.3 %shard_map.473 = (bf16[80,4096]{1,0:T(8,128)(2,1)S(1)}, bf16[80,4096]{1,0:T(8,128)(2,1)S(1)}, bf16[80,4096]{1,0:T(8,128)(2,1)S(1)}) custom-call(s32[8]{0:T(128)S(1)} %warm.1.refs_0_, bf16[80,4096]{1,0:T(8,128)(2,1)S(1)} %copy-done.16, bf16[80,4096]{1,0:T(8,128)(2,1)S(1)} %copy-done.11, bf16[80,4096]{1,0:T(8,128)(2,1)S(1)} %collective-permute-done.6.refs_3_, ...), custom_call_target="tpu_custom_call" | custom-call | flops 4529848320 | bytes 20971520 | tf_op jit(solution)/shard_map/pallas_call | solution.py:272
  138.8 0.9 collective-permute-done.10.refs_3_
  139.7 3.7 %collective-permute-start.12 = (bf16[80,4096]{1,0:T(8,128)(2,1)S(1)}, bf16[80,4096]{1,0:T(8,128)(2,1)S(1)}, u32[]{:S(2)}, u32[]{:S(2)}) collective-permute-start(bf16[80,4096]{1,0:T(8,128)(2,1)S(1)} %get-tuple-element.40), channel_id=1, source_target_pairs={{0,1},{1,2},{2,3},{3,0},{4,5},{5,6},{6,7},{7,4},{8,9},{9,10},{10,1... | collective-permute-start | bytes 1966088 | tf_op jit(solution)/shard_map/ppermute | solution.py:431
  143.6 1.5 collective-permute-start.11
  145.1 1.9 collective-permute-start.13
  147.0 13.8 %shard_map.477 = (bf16[80,4096]{1,0:T(8,128)(2,1)S(1)}, bf16[80,4096]{1,0:T(8,128)(2,1)S(1)}, bf16[80,4096]{1,0:T(8,128)(2,1)S(1)}) custom-call(s32[8]{0:T(128)S(1)} %warm.1.refs_0_, bf16[80,4096]{1,0:T(8,128)(2,1)} %collective-permute-done.16.refs_1_, bf16[80,4096]{1,0:T(8,128)(2,1)S(1)} %collective-permute-done.17.refs_2_, ...), custom_call_target="tpu_custom_call" | custom-call | flops 4529848320 | bytes 20971520 | tf_op jit(solution)/shard_map/pallas_call | solution.py:272
  160.9 1.4 collective-permute-start.30
  162.2 13.3 %shard_map.472 = (bf16[80,4096]{1,0:T(8,128)(2,1)S(1)}, bf16[80,4096]{1,0:T(8,128)(2,1)S(1)}, bf16[80,4096]{1,0:T(8,128)(2,1)S(1)}) custom-call(s32[8]{0:T(128)S(1)} %warm.1.refs_0_, bf16[80,4096]{1,0:T(8,128)(2,1)S(1)} %collective-permute-done.refs_1_, bf16[80,4096]{1,0:T(8,128)(2,1)S(1)} %copy-done.21, bf16[80,4096]{1,0:T(8,128)(2,1)S(1)} %copy-done.23, ...), custom_call_target="tpu_custom_call" | custom-call | flops 4529848320 | bytes 20971520 | tf_op jit(solution)/shard_map/pallas_call | solution.py:272
  175.5 0.8 collective-permute-start.3
  176.3 0.4 shard_map.481
  176.9 0.6 collective-permute-start.31
  177.6 0.5 shard_map.476
  178.0 3.2 %collective-permute-start.14 = (bf16[80,4096]{1,0:T(8,128)(2,1)S(1)}, bf16[80,4096]{1,0:T(8,128)(2,1)S(1)}, u32[]{:S(2)}, u32[]{:S(2)}) collective-permute-start(bf16[80,4096]{1,0:T(8,128)(2,1)S(1)} %get-tuple-element.42), channel_id=1, source_target_pairs={{0,1},{1,2},{2,3},{3,0},{4,5},{5,6},{6,7},{7,4},{8,9},{9,10},{10,1... | collective-permute-start | bytes 1966088 | tf_op jit(solution)/shard_map/ppermute | solution.py:431
  181.2 5.3 %collective-permute-done.30.refs_5_ = bf16[80,4096]{1,0:T(8,128)(2,1)S(1)} collective-permute-done((bf16[80,4096]{1,0:T(8,128)(2,1)S(1)}, bf16[80,4096]{1,0:T(8,128)(2,1)S(1)}, u32[]{:S(2)}, u32[]{:S(2)}) %collective-permute-start.30) | collective-permute-done | bytes 655392 | tf_op jit(solution)/shard_map/ppermute | solution.py:431
  186.6 1.4 collective-permute-start.15
  187.9 9.7 %shard_map.471 = (bf16[80,4096]{1,0:T(8,128)(2,1)S(1)}, bf16[80,4096]{1,0:T(8,128)(2,1)S(1)}) custom-call(s32[8]{0:T(128)S(1)} %warm.1.refs_0_, bf16[80,4096]{1,0:T(8,128)(2,1)S(1)} %shard_map.469.refs_1_, bf16[80,4096]{1,0:T(8,128)(2,1)S(1)} %shard_map.470.refs_2_, bf16[4096,1024]{1,0:T(8,128)(2,1)S(1)} %copy-done.1, bf16[4096,128]{1,0:T(8,128)(2,1)S(1)} %copy-done.4, ...), custom_call_target="tpu_custom_call" | custom-call | flops 3019898880 | bytes 20971520 | tf_op jit(solution)/shard_map/pallas_call | solution.py:272
  197.7 5.4 %collective-permute-done.29.refs_4_ = bf16[80,4096]{1,0:T(8,128)(2,1)S(1)} collective-permute-done((bf16[80,4096]{1,0:T(8,128)(2,1)S(1)}, bf16[80,4096]{1,0:T(8,128)(2,1)S(1)}, u32[]{:S(2)}, u32[]{:S(2)}) %collective-permute-start.29) | collective-permute-done | bytes 655392 | tf_op jit(solution)/shard_map/ppermute | solution.py:431
  203.1 3.1 %shard_map.482.refs_7_ = bf16[160,4096]{1,0:T(8,128)(2,1)} custom-call(s32[8]{0:T(128)S(1)} %warm.1.refs_0_, bf16[160,4096]{1,0:T(8,128)(2,1)} %refs_1_.5, s32[1280,32]{1,0:T(8,128)} %copy.69.refs_8_.refs_9_.refs_2_, bf16[80,4096]{1,0:T(8,128)(2,1)S(1)} %get-tuple-element.44.refs_3_, bf16[80,4096]{1,0:T(8,128)(2,1)S(1)} %collective-permute-done.29.refs_4_, ...), custom_call_target="tpu_custom_call" | custom-call | flops 20971520 | bytes 3932160 | tf_op jit(solution)/shard_map/pallas_call | solution.py:391
  206.2 3.1 %shard_map.483 = bf16[160,4096]{1,0:T(8,128)(2,1)} custom-call(s32[8]{0:T(128)S(1)} %warm.1.refs_0_, bf16[160,4096]{1,0:T(8,128)(2,1)} %refs_1_.5, s32[1280,32]{1,0:T(8,128)} %copy.69.refs_8_.refs_9_.refs_2_, bf16[80,4096]{1,0:T(8,128)(2,1)S(1)} %get-tuple-element.31.refs_3_, ...), custom_call_target="tpu_custom_call", output_to_operand_aliasing={{}: (7, {})} | custom-call | flops 20971520 | bytes 3932160 | tf_op jit(solution)/shard_map/pallas_call | solution.py:391
  (74 shorter events, 1.2 us)
Async XLA Ops:
  0.0 69.9 %copy-start.4 = (bf16[4096,128]{1,0:T(8,128)(2,1)S(1)}, bf16[4096,128]{1,0:T(8,128)(2,1)}, u32[]{:S(2)}) copy-start(bf16[4096,128]{1,0:T(8,128)(2,1)} %refs_4_.13) | copy-start | bytes 3145732
  0.0 69.9 %copy-start.5 = (bf16[4096,128]{1,0:T(8,128)(2,1)S(1)}, bf16[4096,128]{1,0:T(8,128)(2,1)}, u32[]{:S(2)}) copy-start(bf16[4096,128]{1,0:T(8,128)(2,1)} %refs_5_.13) | copy-start | bytes 3145732
  1.9 16.6 %collective-permute-start.16 = (bf16[80,4096]{1,0:T(8,128)(2,1)S(1)}, bf16[80,4096]{1,0:T(8,128)(2,1)}, u32[]{:S(2)}, u32[]{:S(2)}) collective-permute-start(bf16[80,4096]{1,0:T(8,128)(2,1)S(1)} %shard_map.469.refs_1_), channel_id=1, source_target_pairs={{0,1},{1,2},{2,3},{3,0},{4,5},{5,6},{6,7},{7,4},{8,9},{9,10},{10,1... | collective-permute-start | bytes 1966088 | tf_op jit(solution)/shard_map/ppermute | solution.py:431
  2.1 18.0 %collective-permute-start.18 = (bf16[80,4096]{1,0:T(8,128)(2,1)S(1)}, bf16[80,4096]{1,0:T(8,128)(2,1)S(1)}, u32[]{:S(2)}, u32[]{:S(2)}) collective-permute-start(bf16[80,4096]{1,0:T(8,128)(2,1)S(1)} %shard_map.469.refs_1_), channel_id=1, source_target_pairs={{0,4},{1,5},{2,6},{3,7},{4,0},{5,1},{6,2},{7,3},{8,12},{9,13},{10,... | collective-permute-start | bytes 1966088 | tf_op jit(solution)/shard_map/ppermute | solution.py:431
  5.5 17.6 %collective-permute-start.1 = (bf16[80,4096]{1,0:T(8,128)(2,1)S(1)}, bf16[80,4096]{1,0:T(8,128)(2,1)S(1)}, u32[]{:S(2)}, u32[]{:S(2)}) collective-permute-start(bf16[80,4096]{1,0:T(8,128)(2,1)S(1)} %shard_map.470.refs_2_), channel_id=1, source_target_pairs={{0,3},{1,0},{2,1},{3,2},{4,7},{5,4},{6,5},{7,6},{8,11},{9,8},{10,9... | collective-permute-start | bytes 1966088 | tf_op jit(solution)/shard_map/ppermute | solution.py:431
  7.3 26.4 %collective-permute-start.2 = (bf16[80,4096]{1,0:T(8,128)(2,1)S(1)}, bf16[80,4096]{1,0:T(8,128)(2,1)S(1)}, u32[]{:S(2)}, u32[]{:S(2)}) collective-permute-start(bf16[80,4096]{1,0:T(8,128)(2,1)S(1)} %shard_map.470.refs_2_), channel_id=1, source_target_pairs={{0,4},{1,5},{2,6},{3,7},{4,0},{5,1},{6,2},{7,3},{8,12},{9,13},{10,... | collective-permute-start | bytes 1966088 | tf_op jit(solution)/shard_map/ppermute | solution.py:431
  18.6 29.2 %collective-permute-start.19 = (bf16[80,4096]{1,0:T(8,128)(2,1)}, bf16[80,4096]{1,0:T(8,128)(2,1)S(1)}, u32[]{:S(2)}, u32[]{:S(2)}) collective-permute-start(bf16[80,4096]{1,0:T(8,128)(2,1)} %collective-permute-done.16.refs_1_), channel_id=1, source_target_pairs={{0,4},{1,5},{2,6},{3,7},{4,0},{5,1},{6,2},{7,3},{8,12},{9,13},{10,... | collective-permute-start | bytes 1966088 | tf_op jit(solution)/shard_map/ppermute | solution.py:431
  20.1 31.8 %collective-permute-start.20 = (bf16[80,4096]{1,0:T(8,128)(2,1)S(1)}, bf16[80,4096]{1,0:T(8,128)(2,1)S(1)}, u32[]{:S(2)}, u32[]{:S(2)}) collective-permute-start(bf16[80,4096]{1,0:T(8,128)(2,1)S(1)} %collective-permute-done.18.refs_3_), channel_id=1, source_target_pairs={{0,3},{1,0},{2,1},{3,2},{4,7},{5,4},{6,5},{7,6},{8,11},{9,8},{10,9... | collective-permute-start | bytes 1966088 | tf_op jit(solution)/shard_map/ppermute | solution.py:431
  21.6 0.8 copy-start.24
  23.0 44.1 %copy-start.20 = (bf16[80,4096]{1,0:T(8,128)(2,1)}, bf16[80,4096]{1,0:T(8,128)(2,1)S(1)}, u32[]{:S(2)}) copy-start(bf16[80,4096]{1,0:T(8,128)(2,1)S(1)} %collective-permute-done.1.refs_2_) | copy-start | bytes 1966084
  23.0 37.6 %collective-permute-start.5 = (bf16[80,4096]{1,0:T(8,128)(2,1)S(1)}, bf16[80,4096]{1,0:T(8,128)(2,1)S(1)}, u32[]{:S(2)}, u32[]{:S(2)}) collective-permute-start(bf16[80,4096]{1,0:T(8,128)(2,1)S(1)} %collective-permute-done.1.refs_2_), channel_id=1, source_target_pairs={{0,4},{1,5},{2,6},{3,7},{4,0},{5,1},{6,2},{7,3},{8,12},{9,13},{10,... | collective-permute-start | bytes 1966088 | tf_op jit(solution)/shard_map/ppermute | solution.py:431
  33.7 30.2 %collective-permute-start.4 = (bf16[80,4096]{1,0:T(8,128)(2,1)S(1)}, bf16[80,4096]{1,0:T(8,128)(2,1)S(1)}, u32[]{:S(2)}, u32[]{:S(2)}) collective-permute-start(bf16[80,4096]{1,0:T(8,128)(2,1)S(1)} %collective-permute-done.2.refs_3_), channel_id=1, source_target_pairs={{0,1},{1,2},{2,3},{3,0},{4,5},{5,6},{6,7},{7,4},{8,9},{9,10},{10,1... | collective-permute-start | bytes 1966088 | tf_op jit(solution)/shard_map/ppermute | solution.py:431
  35.4 0.9 copy-start.22
  47.8 13.7 %copy-start.12 = (bf16[80,4096]{1,0:T(8,128)(2,1)}, bf16[80,4096]{1,0:T(8,128)(2,1)S(1)}, u32[]{:S(2)}) copy-start(bf16[80,4096]{1,0:T(8,128)(2,1)S(1)} %collective-permute-done.19.refs_1_) | copy-start | bytes 1966084
  48.6 29.7 %collective-permute-start.22 = (bf16[48,4096]{1,0:T(8,128)(2,1)}, bf16[48,4096]{1,0:T(8,128)(2,1)}, u32[]{:S(2)}, u32[]{:S(2)}) collective-permute-start(bf16[48,4096]{1,0:T(8,128)(2,1)} %slice.18), channel_id=1, source_target_pairs={{0,1},{1,2},{2,3},{3,0},{4,5},{5,6},{6,7},{7,4},{8,9},{9,10},{10,1... | collective-permute-start | bytes 1179656 | tf_op jit(solution)/shard_map/ppermute | solution.py:431
  50.3 51.7 %collective-permute-start.21 = (bf16[80,4096]{1,0:T(8,128)(2,1)}, bf16[80,4096]{1,0:T(8,128)(2,1)}, u32[]{:S(2)}, u32[]{:S(2)}) collective-permute-start(bf16[80,4096]{1,0:T(8,128)(2,1)} %collective-permute-done.16.refs_1_), channel_id=1, source_target_pairs={{0,1},{1,2},{2,3},{3,0},{4,5},{5,6},{6,7},{7,4},{8,9},{9,10},{10,1... | collective-permute-start | bytes 1966088 | tf_op jit(solution)/shard_map/ppermute | solution.py:431
  51.9 12.8 %copy-start.17 = (bf16[80,4096]{1,0:T(8,128)(2,1)}, bf16[80,4096]{1,0:T(8,128)(2,1)S(1)}, u32[]{:S(2)}) copy-start(bf16[80,4096]{1,0:T(8,128)(2,1)S(1)} %collective-permute-done.20.refs_2_) | copy-start | bytes 1966084
  52.7 25.2 %collective-permute-start.23 = (bf16[32,4096]{1,0:T(8,128)(2,1)}, bf16[32,4096]{1,0:T(8,128)(2,1)}, u32[]{:S(2)}, u32[]{:S(2)}) collective-permute-start(bf16[32,4096]{1,0:T(8,128)(2,1)} %slice.19), channel_id=1, source_target_pairs={{0,3},{1,0},{2,1},{3,2},{4,7},{5,4},{6,5},{7,6},{8,11},{9,8},{10,9... | collective-permute-start | bytes 786440 | tf_op jit(solution)/shard_map/ppermute | solution.py:431
  61.5 0.9 copy-start.10
  62.3 28.9 %collective-permute-start.8 = (bf16[48,4096]{1,0:T(8,128)(2,1)}, bf16[48,4096]{1,0:T(8,128)(2,1)}, u32[]{:S(2)}, u32[]{:S(2)}) collective-permute-start(bf16[48,4096]{1,0:T(8,128)(2,1)} %slice.17), channel_id=1, source_target_pairs={{0,3},{1,0},{2,1},{3,2},{4,7},{5,4},{6,5},{7,6},{8,11},{9,8},{10,9... | collective-permute-start | bytes 1179656 | tf_op jit(solution)/shard_map/ppermute | solution.py:431
  64.7 0.8 copy-start.15
  65.6 25.1 %collective-permute-start.7 = (bf16[32,4096]{1,0:T(8,128)(2,1)}, bf16[32,4096]{1,0:T(8,128)(2,1)}, u32[]{:S(2)}, u32[]{:S(2)}) collective-permute-start(bf16[32,4096]{1,0:T(8,128)(2,1)} %slice.16), channel_id=1, source_target_pairs={{0,1},{1,2},{2,3},{3,0},{4,5},{5,6},{6,7},{7,4},{8,9},{9,10},{10,1... | collective-permute-start | bytes 786440 | tf_op jit(solution)/shard_map/ppermute | solution.py:431
  69.9 3.4 %copy-start = (bf16[4096,1024]{1,0:T(8,128)(2,1)S(1)}, bf16[4096,1024]{1,0:T(8,128)(2,1)}, u32[]{:S(2)}) copy-start(bf16[4096,1024]{1,0:T(8,128)(2,1)} %refs_3_.7) | copy-start | bytes 25165828
  73.2 3.4 %copy-start.2 = (bf16[1024,4096]{1,0:T(8,128)(2,1)S(1)}, bf16[1024,4096]{1,0:T(8,128)(2,1)}, u32[]{:S(2)}) copy-start(bf16[1024,4096]{1,0:T(8,128)(2,1)} %refs_6_.13) | copy-start | bytes 25165828
  76.6 1.8 copy-start.21
  76.6 3.6 %copy-start.1 = (bf16[4096,1024]{1,0:T(8,128)(2,1)S(1)}, bf16[4096,1024]{1,0:T(8,128)(2,1)}, u32[]{:S(2)}) copy-start(bf16[4096,1024]{1,0:T(8,128)(2,1)} %refs_3_.7) | copy-start | bytes 25165828
  76.6 6.0 %copy-start.3 = (bf16[1024,4096]{1,0:T(8,128)(2,1)S(1)}, bf16[1024,4096]{1,0:T(8,128)(2,1)}, u32[]{:S(2)}) copy-start(bf16[1024,4096]{1,0:T(8,128)(2,1)} %refs_6_.13) | copy-start | bytes 25165828
  76.6 6.0 %copy-start.6 = (bf16[1024,80]{1,0:T(8,128)(2,1)S(1)}, bf16[1024,80]{1,0:T(8,128)(2,1)}, u32[]{:S(2)}) copy-start(bf16[1024,80]{1,0:T(8,128)(2,1)} %constant.29.clone.refs_13_.refs_14_) | copy-start | bytes 491524
  76.6 6.0 %copy-start.7 = (bf16[4,32,1024]{2,1,0:T(8,128)(2,1)S(1)}, bf16[4,32,1024]{2,1,0:T(8,128)(2,1)}, u32[]{:S(2)}) copy-start(bf16[4,32,1024]{2,1,0:T(8,128)(2,1)} %constant.30.clone.refs_14_.refs_15_) | copy-start | bytes 786436
  76.6 6.0 %copy-start.8 = (f32[80,128]{1,0:T(8,128)S(1)}, f32[80,128]{1,0:T(8,128)}, u32[]{:S(2)}) copy-start(f32[80,128]{1,0:T(8,128)} %constant.25.clone.refs_9_.refs_10_) | copy-start | bytes 122884
  76.7 6.0 %copy-start.9 = (f32[80,128]{1,0:T(8,128)S(1)}, f32[80,128]{1,0:T(8,128)}, u32[]{:S(2)}) copy-start(f32[80,128]{1,0:T(8,128)} %constant.26.clone.refs_10_.refs_11_) | copy-start | bytes 122884
  76.7 6.0 %copy-start.14 = (bf16[128,80]{1,0:T(8,128)(2,1)S(1)}, bf16[128,80]{1,0:T(8,128)(2,1)}, u32[]{:S(2)}) copy-start(bf16[128,80]{1,0:T(8,128)(2,1)} %constant.27.clone.refs_11_.refs_12_) | copy-start | bytes 61444
  76.7 6.0 %copy-start.19 = (bf16[80,128]{1,0:T(8,128)(2,1)S(1)}, bf16[80,128]{1,0:T(8,128)(2,1)}, u32[]{:S(2)}) copy-start(bf16[80,128]{1,0:T(8,128)(2,1)} %constant.28.clone.refs_12_.refs_13_) | copy-start | bytes 61444
  77.9 65.7 %collective-permute-start.17 = (bf16[80,4096]{1,0:T(8,128)(2,1)S(1)}, bf16[80,4096]{1,0:T(8,128)(2,1)S(1)}, u32[]{:S(2)}, u32[]{:S(2)}) collective-permute-start(bf16[80,4096]{1,0:T(8,128)(2,1)S(1)} %shard_map.469.refs_1_), channel_id=1, source_target_pairs={{0,3},{1,0},{2,1},{3,2},{4,7},{5,4},{6,5},{7,6},{8,11},{9,8},{10,9... | collective-permute-start | bytes 1966088 | tf_op jit(solution)/shard_map/ppermute | solution.py:431
  78.4 41.2 %collective-permute-start.6 = (bf16[80,4096]{1,0:T(8,128)(2,1)S(1)}, bf16[80,4096]{1,0:T(8,128)(2,1)S(1)}, u32[]{:S(2)}, u32[]{:S(2)}) collective-permute-start(bf16[80,4096]{1,0:T(8,128)(2,1)S(1)} %copy-done.21), channel_id=1, source_target_pairs={{0,3},{1,0},{2,1},{3,2},{4,7},{5,4},{6,5},{7,6},{8,11},{9,8},{10,9... | collective-permute-start | bytes 1966088 | tf_op jit(solution)/shard_map/ppermute | solution.py:431
  90.7 28.7 %collective-permute-start.24 = (bf16[48,4096]{1,0:T(8,128)(2,1)S(1)}, bf16[48,4096]{1,0:T(8,128)(2,1)S(1)}, u32[]{:S(2)}, u32[]{:S(2)}) collective-permute-start(bf16[48,4096]{1,0:T(8,128)(2,1)S(1)} %get-tuple-element.49), channel_id=1, source_target_pairs={{0,3},{1,0},{2,1},{3,2},{4,7},{5,4},{6,5},{7,6},{8,11},{9,8},{10,9... | collective-permute-start | bytes 1179656 | tf_op jit(solution)/shard_map/ppermute | solution.py:431
  91.2 11.1 %copy-start.13 = (bf16[80,4096]{1,0:T(8,128)(2,1)S(1)}, bf16[80,4096]{1,0:T(8,128)(2,1)}, u32[]{:S(2)}) copy-start(bf16[80,4096]{1,0:T(8,128)(2,1)} %copy-done.12) | copy-start | bytes 1966084
  91.2 11.1 %copy-start.18 = (bf16[80,4096]{1,0:T(8,128)(2,1)S(1)}, bf16[80,4096]{1,0:T(8,128)(2,1)}, u32[]{:S(2)}) copy-start(bf16[80,4096]{1,0:T(8,128)(2,1)} %copy-done.17) | copy-start | bytes 1966084
  91.2 25.0 %collective-permute-start.25 = (bf16[32,4096]{1,0:T(8,128)(2,1)S(1)}, bf16[32,4096]{1,0:T(8,128)(2,1)S(1)}, u32[]{:S(2)}, u32[]{:S(2)}) collective-permute-start(bf16[32,4096]{1,0:T(8,128)(2,1)S(1)} %get-tuple-element.50), channel_id=1, source_target_pairs={{0,1},{1,2},{2,3},{3,0},{4,5},{5,6},{6,7},{7,4},{8,9},{9,10},{10,1... | collective-permute-start | bytes 786440 | tf_op jit(solution)/shard_map/ppermute | solution.py:431
  102.0 23.5 %copy-start.11 = (bf16[80,4096]{1,0:T(8,128)(2,1)S(1)}, bf16[80,4096]{1,0:T(8,128)(2,1)}, u32[]{:S(2)}) copy-start(bf16[80,4096]{1,0:T(8,128)(2,1)} %copy-done.10) | copy-start | bytes 1966084
  102.0 23.5 %copy-start.16 = (bf16[80,4096]{1,0:T(8,128)(2,1)S(1)}, bf16[80,4096]{1,0:T(8,128)(2,1)}, u32[]{:S(2)}) copy-start(bf16[80,4096]{1,0:T(8,128)(2,1)} %copy-done.15) | copy-start | bytes 1966084
  102.0 22.1 %collective-permute-start.9 = (bf16[32,4096]{1,0:T(8,128)(2,1)S(1)}, bf16[32,4096]{1,0:T(8,128)(2,1)S(1)}, u32[]{:S(2)}, u32[]{:S(2)}) collective-permute-start(bf16[32,4096]{1,0:T(8,128)(2,1)S(1)} %get-tuple-element.37), channel_id=1, source_target_pairs={{0,3},{1,0},{2,1},{3,2},{4,7},{5,4},{6,5},{7,6},{8,11},{9,8},{10,9... | collective-permute-start | bytes 786440 | tf_op jit(solution)/shard_map/ppermute | solution.py:431
  116.2 27.4 %collective-permute-start = (bf16[80,4096]{1,0:T(8,128)(2,1)S(1)}, bf16[80,4096]{1,0:T(8,128)(2,1)S(1)}, u32[]{:S(2)}, u32[]{:S(2)}) collective-permute-start(bf16[80,4096]{1,0:T(8,128)(2,1)S(1)} %shard_map.470.refs_2_), channel_id=1, source_target_pairs={{0,1},{1,2},{2,3},{3,0},{4,5},{5,6},{6,7},{7,4},{8,9},{9,10},{10,1... | collective-permute-start | bytes 1966088 | tf_op jit(solution)/shard_map/ppermute | solution.py:431
  119.4 25.7 %collective-permute-start.27 = (bf16[80,4096]{1,0:T(8,128)(2,1)S(1)}, bf16[80,4096]{1,0:T(8,128)(2,1)S(1)}, u32[]{:S(2)}, u32[]{:S(2)}) collective-permute-start(bf16[80,4096]{1,0:T(8,128)(2,1)S(1)} %get-tuple-element.52), channel_id=1, source_target_pairs={{0,3},{1,0},{2,1},{3,2},{4,7},{5,4},{6,5},{7,6},{8,11},{9,8},{10,9... | collective-permute-start | bytes 1966088 | tf_op jit(solution)/shard_map/ppermute | solution.py:431
  119.6 20.1 %collective-permute-start.10 = (bf16[48,4096]{1,0:T(8,128)(2,1)S(1)}, bf16[48,4096]{1,0:T(8,128)(2,1)S(1)}, u32[]{:S(2)}, u32[]{:S(2)}) collective-permute-start(bf16[48,4096]{1,0:T(8,128)(2,1)S(1)} %get-tuple-element.38), channel_id=1, source_target_pairs={{0,1},{1,2},{2,3},{3,0},{4,5},{5,6},{6,7},{7,4},{8,9},{9,10},{10,1... | collective-permute-start | bytes 1179656 | tf_op jit(solution)/shard_map/ppermute | solution.py:431
  124.1 22.9 %copy-start.25 = (bf16[80,4096]{1,0:T(8,128)(2,1)S(1)}, bf16[80,4096]{1,0:T(8,128)(2,1)}, u32[]{:S(2)}) copy-start(bf16[80,4096]{1,0:T(8,128)(2,1)} %copy-done.24) | copy-start | bytes 1966084
  124.1 36.7 %collective-permute-start.26 = (bf16[80,4096]{1,0:T(8,128)(2,1)S(1)}, bf16[80,4096]{1,0:T(8,128)(2,1)S(1)}, u32[]{:S(2)}, u32[]{:S(2)}) collective-permute-start(bf16[80,4096]{1,0:T(8,128)(2,1)S(1)} %get-tuple-element.51), channel_id=1, source_target_pairs={{0,4},{1,5},{2,6},{3,7},{4,0},{5,1},{6,2},{7,3},{8,12},{9,13},{10,... | collective-permute-start | bytes 1966088 | tf_op jit(solution)/shard_map/ppermute | solution.py:431
  139.7 37.1 %collective-permute-start.12 = (bf16[80,4096]{1,0:T(8,128)(2,1)S(1)}, bf16[80,4096]{1,0:T(8,128)(2,1)S(1)}, u32[]{:S(2)}, u32[]{:S(2)}) collective-permute-start(bf16[80,4096]{1,0:T(8,128)(2,1)S(1)} %get-tuple-element.40), channel_id=1, source_target_pairs={{0,1},{1,2},{2,3},{3,0},{4,5},{5,6},{6,7},{7,4},{8,9},{9,10},{10,1... | collective-permute-start | bytes 1966088 | tf_op jit(solution)/shard_map/ppermute | solution.py:431
  143.5 31.9 %collective-permute-start.28 = (bf16[80,4096]{1,0:T(8,128)(2,1)S(1)}, bf16[80,4096]{1,0:T(8,128)(2,1)S(1)}, u32[]{:S(2)}, u32[]{:S(2)}) collective-permute-start(bf16[80,4096]{1,0:T(8,128)(2,1)S(1)} %get-tuple-element.53), channel_id=1, source_target_pairs={{0,1},{1,2},{2,3},{3,0},{4,5},{5,6},{6,7},{7,4},{8,9},{9,10},{10,1... | collective-permute-start | bytes 1966088 | tf_op jit(solution)/shard_map/ppermute | solution.py:431
  143.6 33.3 %collective-permute-start.11 = (bf16[80,4096]{1,0:T(8,128)(2,1)S(1)}, bf16[80,4096]{1,0:T(8,128)(2,1)S(1)}, u32[]{:S(2)}, u32[]{:S(2)}) collective-permute-start(bf16[80,4096]{1,0:T(8,128)(2,1)S(1)} %get-tuple-element.39), channel_id=1, source_target_pairs={{0,4},{1,5},{2,6},{3,7},{4,0},{5,1},{6,2},{7,3},{8,12},{9,13},{10,... | collective-permute-start | bytes 1966088 | tf_op jit(solution)/shard_map/ppermute | solution.py:431
  145.1 17.1 %copy-start.23 = (bf16[80,4096]{1,0:T(8,128)(2,1)S(1)}, bf16[80,4096]{1,0:T(8,128)(2,1)}, u32[]{:S(2)}) copy-start(bf16[80,4096]{1,0:T(8,128)(2,1)} %copy-done.22) | copy-start | bytes 1966084
  145.1 32.5 %collective-permute-start.13 = (bf16[80,4096]{1,0:T(8,128)(2,1)S(1)}, bf16[80,4096]{1,0:T(8,128)(2,1)S(1)}, u32[]{:S(2)}, u32[]{:S(2)}) collective-permute-start(bf16[80,4096]{1,0:T(8,128)(2,1)S(1)} %get-tuple-element.41), channel_id=1, source_target_pairs={{0,3},{1,0},{2,1},{3,2},{4,7},{5,4},{6,5},{7,6},{8,11},{9,8},{10,9... | collective-permute-start | bytes 1966088 | tf_op jit(solution)/shard_map/ppermute | solution.py:431
  160.9 25.7 %collective-permute-start.30 = (bf16[80,4096]{1,0:T(8,128)(2,1)S(1)}, bf16[80,4096]{1,0:T(8,128)(2,1)S(1)}, u32[]{:S(2)}, u32[]{:S(2)}) collective-permute-start(bf16[80,4096]{1,0:T(8,128)(2,1)S(1)} %get-tuple-element.55), channel_id=1, source_target_pairs={{0,1},{1,2},{2,3},{3,0},{4,5},{5,6},{6,7},{7,4},{8,9},{9,10},{10,1... | collective-permute-start | bytes 1966088 | tf_op jit(solution)/shard_map/ppermute | solution.py:431
  175.5 30.7 %collective-permute-start.3 = (bf16[80,4096]{1,0:T(8,128)(2,1)S(1)}, bf16[80,4096]{1,0:T(8,128)(2,1)S(1)}, u32[]{:S(2)}, u32[]{:S(2)}) collective-permute-start(bf16[80,4096]{1,0:T(8,128)(2,1)S(1)} %get-tuple-element.32), channel_id=1, source_target_pairs={{0,3},{1,0},{2,1},{3,2},{4,7},{5,4},{6,5},{7,6},{8,11},{9,8},{10,9... | collective-permute-start | bytes 1966088 | tf_op jit(solution)/shard_map/ppermute | solution.py:431
  176.8 26.3 %collective-permute-start.29 = (bf16[80,4096]{1,0:T(8,128)(2,1)S(1)}, bf16[80,4096]{1,0:T(8,128)(2,1)S(1)}, u32[]{:S(2)}, u32[]{:S(2)}) collective-permute-start(bf16[80,4096]{1,0:T(8,128)(2,1)S(1)} %get-tuple-element.54), channel_id=1, source_target_pairs={{0,3},{1,0},{2,1},{3,2},{4,7},{5,4},{6,5},{7,6},{8,11},{9,8},{10,9... | collective-permute-start | bytes 1966088 | tf_op jit(solution)/shard_map/ppermute | solution.py:431
  176.9 26.2 %collective-permute-start.31 = (bf16[80,4096]{1,0:T(8,128)(2,1)S(1)}, bf16[80,4096]{1,0:T(8,128)(2,1)S(1)}, u32[]{:S(2)}, u32[]{:S(2)}) collective-permute-start(bf16[80,4096]{1,0:T(8,128)(2,1)S(1)} %get-tuple-element.56), channel_id=1, source_target_pairs={{0,4},{1,5},{2,6},{3,7},{4,0},{5,1},{6,2},{7,3},{8,12},{9,13},{10,... | collective-permute-start | bytes 1966088 | tf_op jit(solution)/shard_map/ppermute | solution.py:431
  178.0 28.2 %collective-permute-start.14 = (bf16[80,4096]{1,0:T(8,128)(2,1)S(1)}, bf16[80,4096]{1,0:T(8,128)(2,1)S(1)}, u32[]{:S(2)}, u32[]{:S(2)}) collective-permute-start(bf16[80,4096]{1,0:T(8,128)(2,1)S(1)} %get-tuple-element.42), channel_id=1, source_target_pairs={{0,1},{1,2},{2,3},{3,0},{4,5},{5,6},{6,7},{7,4},{8,9},{9,10},{10,1... | collective-permute-start | bytes 1966088 | tf_op jit(solution)/shard_map/ppermute | solution.py:431
  186.6 19.7 %collective-permute-start.15 = (bf16[80,4096]{1,0:T(8,128)(2,1)S(1)}, bf16[80,4096]{1,0:T(8,128)(2,1)S(1)}, u32[]{:S(2)}, u32[]{:S(2)}) collective-permute-start(bf16[80,4096]{1,0:T(8,128)(2,1)S(1)} %get-tuple-element.43), channel_id=1, source_target_pairs={{0,4},{1,5},{2,6},{3,7},{4,0},{5,1},{6,2},{7,3},{8,12},{9,13},{10,... | collective-permute-start | bytes 1966088 | tf_op jit(solution)/shard_map/ppermute | solution.py:431
